TPU v7x, 32 devices: a whole 2x2x4 slice. The times are simulated.
32 devices in a mesh: dp: 2 (over x), tx: 4 (over z), ty: 4 (over y, core).
Axes of the slice: x: 2, y: 2, z: 4, core: 2. Of those that a mesh axis runs over, the one named last changes fastest.
Arguments:
- residual: float32 [256, 4096], P('dp', 'tx'), parts along dimension 0
- norm_w: float32 [2, 4096], P(None, 'tx')
- w_in: bfloat16 [2, 4096, 2, 8192], P(None, 'tx', None, 'ty')
- conv_w: float32 [2, 8192, 4], P(None, 'ty')
- conv_b: float32 [2, 8192], P(None, 'ty')
- w_x: bfloat16 [2, 8192, 288], P(None, 'ty')
- w_dt: bfloat16 [2, 256, 8192], P(None, None, 'ty')
- dt_bias: float32 [2, 8192], P(None, 'ty')
- a_log: float32 [2, 8192, 16], P(None, 'ty')
- d_skip: float32 [2, 8192], P(None, 'ty')
- w_out: bfloat16 [2, 8192, 4096], P(None, 'ty', 'tx')
- conv_state: bfloat16 [2, 256, 8192, 3], P(None, ('dp', 'tx'), 'ty'), parts along dimension 1
- ssm_state: float32 [2, 256, 8192, 16], P(None, ('dp', 'tx'), 'ty'), parts along dimension 1
Outputs:
- output 1: float32 [256, 4096], P('dp', 'tx'), parts along dimension 0
- output 2: bfloat16 [2, 256, 8192, 3], P(None, ('dp', 'tx'), 'ty'), parts along dimension 1
- output 3: float32 [2, 256, 8192, 16], P(None, ('dp', 'tx'), 'ty'), parts along dimension 1
There are 2 independent parts. A program takes and returns all parts, laid end to end along the dimension named above; an argument that names none is the same for every part.
All inputs are finite; a program needn't handle non-finite values.
Results may differ from a plain program's by a relative error of at most 0.0151635.
Values are sent between devices in bfloat16 or wider.
A program may use at most 1 GiB of HBM per device.

v0:
```python
import jax
import jax.numpy as jnp
from jax import lax
from jax.sharding import PartitionSpec as P

NORM_EPS = 1e-5
INNER_EPS = 1e-6


def unit_rms(vec):
    return vec * lax.rsqrt(jnp.mean(vec * vec, axis=-1, keepdims=True) + INNER_EPS)


def channel_update(x_branch, z_branch, conv_prev, ssm_prev, conv_w, conv_b, w_x, w_dt, dt_bias, a_log, d_skip, reduce_fn):
    n_rank = w_dt.shape[0]
    n_state = a_log.shape[-1]
    window = jnp.concatenate([conv_prev, x_branch[:, :, None]], axis=-1)
    conv_val = jnp.sum(window.astype(jnp.float32) * conv_w, axis=-1) + conv_b
    x_conv = jax.nn.silu(conv_val).astype(jnp.bfloat16)
    x_dbl = reduce_fn(jnp.dot(x_conv, w_x, preferred_element_type=jnp.float32))
    dt_low = unit_rms(x_dbl[:, :n_rank])
    b_mat = unit_rms(x_dbl[:, n_rank:n_rank + n_state])
    c_mat = unit_rms(x_dbl[:, n_rank + n_state:])
    delta = jax.nn.softplus(jnp.dot(dt_low.astype(jnp.bfloat16), w_dt, preferred_element_type=jnp.float32) + dt_bias)
    x_float = x_conv.astype(jnp.float32)
    decay = jnp.exp(delta[:, :, None] * -jnp.exp(a_log))
    ssm_new = decay * ssm_prev + (delta * x_float)[:, :, None] * b_mat[:, None, :]
    state_val = jnp.sum(ssm_new * c_mat[:, None, :], axis=-1)
    gated = ((state_val + d_skip * x_float) * jax.nn.silu(z_branch.astype(jnp.float32))).astype(jnp.bfloat16)
    return gated, window[:, :, 1:], ssm_new


def solution(mesh):
    n_dmod = mesh.shape["tx"]

    def sum_over_ty(part_sum):
        return lax.psum(part_sum.astype(jnp.bfloat16), "ty").astype(jnp.float32)

    def local_step(residual, norm_w, w_in, conv_w, conv_b, w_x, w_dt, dt_bias, a_log, d_skip, w_out, conv_state, ssm_state):
        d_model = residual.shape[1] * n_dmod
        conv_list = []
        ssm_list = []
        for layer_idx in range(norm_w.shape[0]):
            sq_part = jnp.sum(residual * residual, axis=-1, keepdims=True)
            sq_total = lax.psum(sq_part, "tx")
            normed = (residual * lax.rsqrt(sq_total / d_model + NORM_EPS) * norm_w[layer_idx]).astype(jnp.bfloat16)
            proj_part = jnp.einsum("bd,dke->bke", normed, w_in[layer_idx], preferred_element_type=jnp.float32)
            proj_in = lax.psum_scatter(proj_part.astype(jnp.bfloat16), "tx", scatter_dimension=0, tiled=True)
            gated, conv_new, ssm_new = channel_update(proj_in[:, 0, :], proj_in[:, 1, :], conv_state[layer_idx], ssm_state[layer_idx], conv_w[layer_idx], conv_b[layer_idx], w_x[layer_idx], w_dt[layer_idx], dt_bias[layer_idx], a_log[layer_idx], d_skip[layer_idx], sum_over_ty)
            gated_rows = lax.all_gather(gated, "tx", axis=0, tiled=True)
            out_part = jnp.dot(gated_rows, w_out[layer_idx], preferred_element_type=jnp.float32)
            residual = residual + sum_over_ty(out_part)
            conv_list.append(conv_new)
            ssm_list.append(ssm_new)
        return residual, jnp.stack(conv_list), jnp.stack(ssm_list)

    cache_spec = P(None, ("dp", "tx"), "ty", None)
    in_specs = (P("dp", "tx"), P(None, "tx"), P(None, "tx", None, "ty"), P(None, "ty", None), P(None, "ty"), P(None, "ty", None), P(None, None, "ty"), P(None, "ty"), P(None, "ty", None), P(None, "ty"), P(None, "ty", "tx"), cache_spec, cache_spec)
    out_specs = (P("dp", "tx"), cache_spec, cache_spec)
    return jax.shard_map(local_step, mesh=mesh, in_specs=in_specs, out_specs=out_specs, check_vma=False)
```

profile of v0, /device:TPU:0, one launch (start us, length us, event | category | flops | bytes accessed | tf_op | source)
XLA Modules:
  0.0 269.7 jit_solution(4069292104598865785)
XLA Ops:
  7.2 14.3 %fusion.68 = (bf16[1,1024,2,2048]{3,2,1,0:T(2,128)(2,1)}, bf16[1,1024,2,2048]{3,2,1,0:T(2,128)(2,1)}) fusion(bf16[2,1024,2,2048]{3,2,1,0:T(2,128)(2,1)} %param.15), kind=kLoop, calls=%fused_computation.120 | loop fusion | bytes 33554432 | tf_op jit(solution)/shard_map/slice | solution.py:47
  21.7 13.5 %psum.42 = f32[128,1]{0,1:T(1,128)S(1)} all-reduce(f32[128,1]{0,1:T(1,128)S(1)} %bitcast.126), channel_id=1, replica_groups=mesh['dp'=2,'tx'=4,'ty'=4] {'tx'}, use_global_device_ids=true, to_apply=%region_1.0 | all-reduce | flops 128 | bytes 1024 | tf_op jit(solution)/shard_map/psum | solution.py:45
  35.3 9.8 %fusion.14 = bf16[128,2,2048]{2,0,1:T(8,128)(2,1)} fusion(bf16[1,1024,2,2048]{3,2,1,0:T(2,128)(2,1)} %get-tuple-element.7, f32[128,1024]{1,0:T(8,128)S(1)} %copy-done, f32[1024]{0:T(1024)S(1)} %bitcast.125, f32[128]{0:T(128)S(1)} %rsqrt_bitcast_fusion.1), kind=kOutput, calls=%fused_computation.21 | convolution fusion | flops 1074659328 | bytes 9966080 | tf_op jit(solution)/shard_map/bd,dke->bke/dot_general | solution.py:47
  45.4 25.4 %reduce-scatter.3.cloned.1.call-done = bf16[32,2,2048]{2,0,1:T(8,128)(2,1)} async-done(((bf16[128,2,2048]{2,0,1:T(8,128)(2,1)}), bf16[32,2,2048]{2,0,1:T(8,128)(2,1)}) %reduce-scatter.3.cloned.1.call-update) | async-done | bytes 262160 | tf_op jit(solution)/shard_map/reduce_scatter | solution.py:48
  71.8 1.7 fusion.28
  73.6 10.4 %psum.43 = bf16[32,288]{1,0:T(8,128)(2,1)S(1)} all-reduce(bf16[32,288]{1,0:T(8,128)(2,1)S(1)} %fusion.28), channel_id=1, replica_groups=mesh['dp'=2,'tx'=4,'ty'=4] {'ty'}, use_global_device_ids=true, to_apply=%region_4.5 | all-reduce | flops 9216 | bytes 36864 | tf_op jit(solution)/shard_map/psum | solution.py:37
  84.4 1.7 convert_multiply_fusion.5
  86.1 3.4 %fusion.11 = f32[32,2048]{1,0:T(8,128)S(1)} fusion(f32[2,32,2048,16]{2,3,1,0:T(8,128)} %param.25, f32[32,16]{1,0:T(8,128)S(1)} %get-tuple-element.20, f32[32,16]{1,0:T(8,128)S(1)} %get-tuple-element.19, f32[32,2048]{1,0:T(8,128)S(1)} %get-tuple-element.29, f32[2048,16]{0,1:T(8,128)S(1)} %get-tuple-element.14, f32[32,2048]{1,0:T(8,128)S(1)} %get-tuple-element.30), kind=kLoop, calls=%fused_computation.16 | loop fusion | flops 6225920 | bytes 5115904 | tf_op jit(solution)/shard_map/reduce_sum | solution.py:28
  89.7 16.2 %all_gather.6 = bf16[128,2048]{1,0:T(8,128)(2,1)S(1)} all-gather(bf16[32,2048]{1,0:T(8,128)(2,1)S(1)} %fusion.44), channel_id=1, replica_groups=mesh['dp'=2,'tx'=4,'ty'=4] {'tx'}, dimensions={0}, use_global_device_ids=true | all-gather | bytes 655360 | tf_op jit(solution)/shard_map/all_gather | solution.py:50
  105.9 3.6 %fusion.16 = bf16[128,1024]{1,0:T(8,128)(2,1)} fusion(bf16[128,2048]{1,0:T(8,128)(2,1)S(1)} %all_gather.6, bf16[2,2048,1024]{2,1,0:T(8,128)(2,1)} %param.23), kind=kOutput, calls=%fused_computation.25 | convolution fusion | flops 537001984 | bytes 4980736 | tf_op jit(solution)/shard_map/dot_general | solution.py:51
  109.6 30.4 %all-reduce.3.cloned.1.call-done = bf16[128,1024]{1,0:T(8,128)(2,1)} async-done(((bf16[128,1024]{1,0:T(8,128)(2,1)}), bf16[128,1024]{1,0:T(8,128)(2,1)}) %all-reduce.3.cloned.1.call-update) | async-done | bytes 262160 | tf_op jit(solution)/shard_map/psum | solution.py:37
  141.1 11.9 %psum.45 = f32[128,1]{0,1:T(1,128)S(1)} all-reduce(f32[128,1]{0,1:T(1,128)S(1)} %bitcast.127), channel_id=1, replica_groups=mesh['dp'=2,'tx'=4,'ty'=4] {'tx'}, use_global_device_ids=true, to_apply=%region_11.12 | all-reduce | flops 128 | bytes 1024 | tf_op jit(solution)/shard_map/psum | solution.py:45
  153.0 9.7 %fusion.15 = bf16[128,2,2048]{2,0,1:T(8,128)(2,1)} fusion(bf16[1,1024,2,2048]{3,2,1,0:T(2,128)(2,1)} %get-tuple-element.8, f32[1024]{0:T(1024)S(1)} %bitcast.124, f32[128]{0:T(128)S(1)} %rsqrt_bitcast_fusion, f32[128,1024]{1,0:T(8,128)S(1)} %copy-done, bf16[128,1024]{1,0:T(8,128)(2,1)} %all-reduce.3.cloned.1.call-done), kind=kOutput, calls=%fused_computation.22 | convolution fusion | flops 1074921472 | bytes 10228224 | tf_op jit(solution)/shard_map/bd,dke->bke/dot_general | solution.py:47
  162.8 24.6 %reduce-scatter.5.cloned.1.call-done = bf16[32,2,2048]{2,0,1:T(8,128)(2,1)} async-done(((bf16[128,2,2048]{2,0,1:T(8,128)(2,1)}), bf16[32,2,2048]{2,0,1:T(8,128)(2,1)}) %reduce-scatter.5.cloned.1.call-update) | async-done | bytes 262160 | tf_op jit(solution)/shard_map/reduce_scatter | solution.py:48
  188.4 1.7 fusion.31
  190.2 10.3 %psum.46 = bf16[32,288]{1,0:T(8,128)(2,1)S(1)} all-reduce(bf16[32,288]{1,0:T(8,128)(2,1)S(1)} %fusion.31), channel_id=1, replica_groups=mesh['dp'=2,'tx'=4,'ty'=4] {'ty'}, use_global_device_ids=true, to_apply=%region_14.15 | all-reduce | flops 9216 | bytes 36864 | tf_op jit(solution)/shard_map/psum | solution.py:37
  201.0 1.8 convert_multiply_fusion.3
  202.8 8.3 %multiply_add_fusion.1 = (f32[1,32,2048,16]{2,3,1,0:T(8,128)}, f32[1,32,2048,16]{2,3,1,0:T(8,128)}) fusion(f32[2,32,2048,16]{2,3,1,0:T(8,128)} %param.25, f32[32,16]{1,0:T(8,128)S(1)} %get-tuple-element.19, f32[32,2048]{1,0:T(8,128)S(1)} %get-tuple-element.29, f32[2048,16]{0,1:T(8,128)S(1)} %get-tuple-element.14, f32[32,2048]{1,0:T(8,128)S(1)} %get-tuple-element.30, ...), kind=kLoop, calls=%fused_computation.18 | loop fusion | flops 8388608 | bytes 18092032 | tf_op jit(solution)/shard_map/add | solution.py:27
  211.1 1.9 fusion.6
  213.2 16.2 %all_gather.7 = bf16[128,2048]{1,0:T(8,128)(2,1)S(1)} all-gather(bf16[32,2048]{1,0:T(8,128)(2,1)S(1)} %fusion.47), channel_id=1, replica_groups=mesh['dp'=2,'tx'=4,'ty'=4] {'tx'}, dimensions={0}, use_global_device_ids=true | all-gather | bytes 655360 | tf_op jit(solution)/shard_map/all_gather | solution.py:50
  229.5 1.4 fusion.19
  230.9 8.0 %pad_maximum_fusion = f32[2,32,2048,16]{2,3,1,0:T(8,128)} fusion(f32[1,32,2048,16]{2,3,1,0:T(8,128)} %get-tuple-element.10, f32[1,32,2048,16]{2,3,1,0:T(8,128)} %get-tuple-element.9), kind=kLoop, calls=%fused_computation | loop fusion | flops 2097152 | bytes 16777216 | tf_op jit(solution)/shard_map/stack | solution.py:55
  239.9 21.5 %all-reduce.5.cloned.1.call-done = bf16[128,1024]{1,0:T(8,128)(2,1)} async-done(((bf16[128,1024]{1,0:T(8,128)(2,1)}), bf16[128,1024]{1,0:T(8,128)(2,1)}) %all-reduce.5.cloned.1.call-update) | async-done | bytes 262160 | tf_op jit(solution)/shard_map/psum | solution.py:37
  261.4 1.8 convert_add_fusion
  (73 shorter events, 5.9 us)
Async XLA Ops:
  7.2 14.4 %copy-start.10 = (f32[2,1024]{1,0:T(2,128)S(1)}, f32[2,1024]{1,0:T(2,128)}, u32[]{:S(2)}) copy-start(f32[2,1024]{1,0:T(2,128)} %param.14) | copy-start | bytes 24580
  7.2 14.4 %copy-start = (f32[128,1024]{1,0:T(8,128)S(1)}, f32[128,1024]{1,0:T(8,128)}, u32[]{:S(2)}) copy-start(f32[128,1024]{1,0:T(8,128)} %param.13) | copy-start | bytes 1572868
  7.2 63.6 %reduce-scatter.3.cloned.1.call-start = ((), (), s32[]{:S(2)}) async-start(), calls=%async_computation.2 | async-start | bytes 1310720 | tf_op jit(solution)/shard_map/reduce_scatter | solution.py:48
  35.2 9.9 %copy-start.7 = (f32[2,2048]{1,0:T(2,128)S(1)}, f32[2,2048]{1,0:T(2,128)}, u32[]{:S(2)}) copy-start(f32[2,2048]{1,0:T(2,128)} %param.17) | copy-start | bytes 49156
  35.2 10.0 %copy-start.8 = (f32[2,2048]{1,0:T(2,128)S(1)}, f32[2,2048]{1,0:T(2,128)}, u32[]{:S(2)}) copy-start(f32[2,2048]{1,0:T(2,128)} %param.20) | copy-start | bytes 49156
  35.2 10.0 %copy-start.9 = (f32[2,2048]{1,0:T(2,128)S(1)}, f32[2,2048]{1,0:T(2,128)}, u32[]{:S(2)}) copy-start(f32[2,2048]{1,0:T(2,128)} %param.22) | copy-start | bytes 49156
  35.2 10.0 %copy-start.6 = (f32[2,2048,4]{1,2,0:T(4,128)S(1)}, f32[2,2048,4]{1,2,0:T(4,128)}, u32[]{:S(2)}) copy-start(f32[2,2048,4]{1,2,0:T(4,128)} %param.16) | copy-start | bytes 196612
  35.3 10.0 %copy-start.5 = (f32[2,2048,16]{1,2,0:T(8,128)S(1)}, f32[2,2048,16]{1,2,0:T(8,128)}, u32[]{:S(2)}) copy-start(f32[2,2048,16]{1,2,0:T(8,128)} %param.21) | copy-start | bytes 786436
  35.3 10.1 %copy-start.2 = (bf16[2,32,2048,3]{2,1,3,0:T(8,128)(2,1)S(1)}, bf16[2,32,2048,3]{2,1,3,0:T(8,128)(2,1)}, u32[]{:S(2)}) copy-start(bf16[2,32,2048,3]{2,1,3,0:T(8,128)(2,1)} %param.24) | copy-start | bytes 2359300
  45.1 94.9 %all-reduce.3.cloned.1.call-start = ((), (), s32[]{:S(2)}) async-start(), calls=%async_computation.3 | async-start | bytes 524288 | tf_op jit(solution)/shard_map/psum | solution.py:37
  73.6 15.9 %copy-start.4 = (bf16[32,2,2048]{2,0,1:T(8,128)(2,1)S(1)}, bf16[32,2,2048]{2,0,1:T(8,128)(2,1)}, u32[]{:S(2)}) copy-start(bf16[32,2,2048]{2,0,1:T(8,128)(2,1)} %reduce-scatter.3.cloned.1.call-done) | copy-start | bytes 786436
  109.6 77.8 %reduce-scatter.5.cloned.1.call-start = ((), (), s32[]{:S(2)}) async-start(), calls=%async_computation.4 | async-start | bytes 1310720 | tf_op jit(solution)/shard_map/reduce_scatter | solution.py:48
  162.7 98.7 %all-reduce.5.cloned.1.call-start = ((), (), s32[]{:S(2)}) async-start(), calls=%async_computation.5 | async-start | bytes 524288 | tf_op jit(solution)/shard_map/psum | solution.py:37
  200.9 10.1 %slice-start = ((s8[8388608]{0:T(1024)(128)(4,1)}), s8[4194304]{0:T(1024)(128)(4,1)S(1)}, s32[]{:S(2)}) async-start(s8[8388608]{0:T(1024)(128)(4,1)} %bitcast.112), calls=%async_computation.6 | async-start | bytes 8388608
  201.0 28.5 %slice-start.2 = ((s8[8388608]{0:T(1024)(128)(4,1)}), s8[4194304]{0:T(1024)(128)(4,1)S(1)}, s32[]{:S(2)}) async-start(s8[8388608]{0:T(1024)(128)(4,1)} %bitcast.128), calls=%async_computation.8 | async-start | bytes 8388608
  202.8 8.3 %slice-start.1 = ((s8[8388608]{0:T(1024)(128)(4,1)}), s8[4194304]{0:T(1024)(128)(4,1)S(1)}, s32[]{:S(2)}) async-start(s8[8388608]{0:T(1024)(128)(4,1)} %bitcast.112), calls=%async_computation.7 | async-start | bytes 8388608
  202.8 26.7 %slice-start.3 = ((s8[8388608]{0:T(1024)(128)(4,1)}), s8[4194304]{0:T(1024)(128)(4,1)S(1)}, s32[]{:S(2)}) async-start(s8[8388608]{0:T(1024)(128)(4,1)} %bitcast.128), calls=%async_computation.9 | async-start | bytes 8388608
  211.1 2.0 copy-start.3
  230.9 30.4 %copy-start.1 = (bf16[128,1024]{1,0:T(8,128)(2,1)S(1)}, bf16[128,1024]{1,0:T(8,128)(2,1)}, u32[]{:S(2)}) copy-start(bf16[128,1024]{1,0:T(8,128)(2,1)} %all-reduce.3.cloned.1.call-done) | copy-start | bytes 786436
Sparse Core Ops, SparseCore 0:
  45.2 25.5 reduce-scatter.2
  109.7 30.2 all-reduce.2
  162.8 24.5 reduce-scatter.4
  231.1 30.2 all-reduce.4
where the time goes:
time: 270 us
  waiting for transfers between devices  102 us (38%)
  blocking collectives  78.5 us (29%)
  matrix products  31.6 us (12%)
  other arithmetic  27.1 us (10%)
  local copies, waits for them, and re-layouts  16.3 us (6%)
  between operations  14.2 us (5%)
    psum x2, waiting for transfers between devices, sum_over_ty(): return lax.psum(part_sum.astype(jnp.bfloat16), 'ty').astype(jnp.float32)  51.8 us
    reduce_scatter x2, waiting for transfers between devices, local_step(): lax.psum_scatter(proj_part.astype(jnp.bfloat16), 'tx', scatter_dimension=...  49.9 us
    all_gather x2, blocking collectives, local_step(): gated_rows = lax.all_gather(gated, 'tx', axis=0, tiled=True)  32.5 us
    psum x2, blocking collectives, local_step(): sq_total = lax.psum(sq_part, 'tx')  25.4 us
    psum x2, blocking collectives, sum_over_ty(): return lax.psum(part_sum.astype(jnp.bfloat16), 'ty').astype(jnp.float32)  20.7 us
    dot_general x2, matrix products, local_step(): jnp.einsum('bd,dke->bke', normed, w_in[layer_idx], preferred_element_type...  19.5 us
    slice x1, local copies, waits for them, and re-layouts, local_step(): w_in[layer_idx]  14.3 us
    another operation x4, other arithmetic, local_step(): return (residual, jnp.stack(conv_list), jnp.stack(ssm_list))  9.03 us
  transfers between devices with their start and end apart: 4, of which 4 were waited for; matrix products, arithmetic and copies ran while one was open for 3% of the time, Pallas kernels for 0%

commit v1 on v0

v1 whole, which is shorter than its diff:
```python
import jax
import jax.numpy as jnp
from jax import lax
from jax.experimental import pallas as pl
from jax.experimental.pallas import tpu as pltpu
from jax.sharding import PartitionSpec as P

NORM_EPS = 1e-5
INNER_EPS = 1e-6
LOG2E = 1.4426950408889634
BF16, F32 = jnp.bfloat16, jnp.float32
MESH = pl.DeviceIdType.MESH
ANY = pl.BlockSpec(memory_space=pl.ANY)


def dot(a, b):
    return jnp.dot(a, b, preferred_element_type=F32)


def make_kernel(n_layer, n_tx, n_ty, rows, d_loc, chan, rank, n_state, chunk):
    blk = rows // n_tx
    half = rows // 2
    n_c = chan // chunk
    d_model = d_loc * n_tx
    n_q = 4
    qw = d_loc // n_q
    n_w = chan // 128
    last = n_tx - 1

    def kernel(
        r_hbm, nw_hbm, win_hbm, cw_hbm, cb_hbm, wx_hbm, wdt_hbm, db_hbm, al_hbm, ds_hbm, wout_hbm, cs_hbm, ss_hbm,
        r_out, conv_out, ssm_out,
        r, nw, win, cw, cb, wx, wdt, db, al, ds, wout, cs, ss,
        hx, own, rup, rdn, uf, xi, xc, dt, dx, sv, bc, pown, pin, yall, acc, s1o, s1i, s2o, s2i, s3o, s3i, sto, sti,
        ld_sem, win_sem, out_sem, ssm_sem, up_s, up_r, dn_s, dn_r, p_s, p_r, ag_s, ag_r, s_s, s_r, st_s, st_r,
    ):
        dp, me, ty = lax.axis_index("dp"), lax.axis_index("tx"), lax.axis_index("ty")
        core = lax.rem(ty, 2)
        barrier = pltpu.get_barrier_semaphore()
        tx_of = lambda k: (dp, k, ty)
        ty_of = lambda k: (dp, me, k)

        loads = {}
        names = dict(r=(r_hbm, r), nw=(nw_hbm, nw), cw=(cw_hbm, cw), cb=(cb_hbm, cb), db=(db_hbm, db), al=(al_hbm, al), ds=(ds_hbm, ds), cs=(cs_hbm, cs))
        for k, key in enumerate(names):
            loads[key] = pltpu.make_async_copy(names[key][0], names[key][1], ld_sem.at[k])
        for l in range(n_layer):
            for k, (key, src, dst) in enumerate((("wx", wx_hbm, wx), ("wdt", wdt_hbm, wdt), ("wout", wout_hbm, wout), ("ss", ss_hbm, ss))):
                loads[key, l] = pltpu.make_async_copy(src.at[l], dst.at[l], ld_sem.at[len(names) + 4 * l + k])
            for t in range(n_w):
                loads["win", l, t] = pltpu.make_async_copy(win_hbm.at[l, :, :, pl.ds(t * 128, 128)], win.at[l, t], win_sem.at[l, t])

        def start(*keys):
            for key in keys:
                loads[key].start()

        def wait(*keys):
            for key in keys:
                loads[key].wait()

        start("r", "nw")
        start(*[("win", 0, t) for t in range(n_w)])
        for k in range(1, n_tx):
            pl.semaphore_signal(barrier, 1, device_id=tx_of(lax.rem(me + k, n_tx)), device_id_type=MESH)
        for k in range(1, n_ty):
            pl.semaphore_signal(barrier, 1, device_id=ty_of(lax.rem(ty + k, n_ty)), device_id_type=MESH)
        start("cw", "cb", "db", "al", "ds", "cs", ("wx", 0))

        def remote(src, dst, ssem, rsem, dev):
            return pltpu.make_async_remote_copy(src_ref=src, dst_ref=dst, send_sem=ssem, recv_sem=rsem, device_id=dev, device_id_type=MESH)

        def up_copy(l, c, b):
            return remote(own.at[l, c, b], rup.at[l, c, b], up_s.at[l, c, b], up_r.at[l, c, b], tx_of(jnp.minimum(me + 1, last)))

        def dn_copy(l, c, b):
            return remote(own.at[l, c, b], rdn.at[l, c, b], dn_s.at[l, c, b], dn_r.at[l, c, b], tx_of(jnp.maximum(me - 1, 0)))

        def forward(l, c):
            for j in range(last, 0, -1):
                @pl.when(me + j <= last)
                def _():
                    b = me + j
                    @pl.when(me > 0)
                    def _():
                        up_copy(l, c, b).wait_recv()
                        own[l, c, b] = (own[l, c, b].astype(F32) + rup[l, c, b].astype(F32)).astype(BF16)
                    up_copy(l, c, b).start()

                @pl.when(me - j >= 0)
                def _():
                    b = me - j
                    @pl.when(me < last)
                    def _():
                        dn_copy(l, c, b).wait_recv()
                        own[l, c, b] = (own[l, c, b].astype(F32) + rdn[l, c, b].astype(F32)).astype(BF16)
                    dn_copy(l, c, b).start()

        def forward_end(l, c):
            for j in range(last, 0, -1):
                @pl.when(me + j <= last)
                def _():
                    up_copy(l, c, me + j).wait_send()

                @pl.when(me - j >= 0)
                def _():
                    dn_copy(l, c, me - j).wait_send()

        def finish(l, c):
            uf[...] = own[l, c, me].astype(F32)

            @pl.when(me > 0)
            def _():
                up_copy(l, c, me).wait_recv()
                uf[...] += rup[l, c, me].astype(F32)

            @pl.when(me < last)
            def _():
                dn_copy(l, c, me).wait_recv()
                uf[...] += rdn[l, c, me].astype(F32)
            return uf[...].astype(BF16)

        def stat_copy(l, k):
            return remote(sto.at[l], sti.at[l, me], st_s.at[l, k], st_r.at[l, me], tx_of(k))

        def stat_recv(l, k):
            return remote(sto.at[l], sti.at[l, k], st_s.at[l, k], st_r.at[l, k], tx_of(k))

        def p_copy(l, k):
            return remote(pown.at[l], pin.at[l, ty], p_s.at[l, k], p_r.at[l, ty], ty_of(k))

        def p_recv(l, k):
            return remote(pown.at[l], pin.at[l, k], p_s.at[l, k], p_r.at[l, k], ty_of(k))

        def ag_up(l, c, b):
            return remote(yall.at[l, c, b], yall.at[l, c, b], ag_s.at[l, c, 0, b], ag_r.at[l, c, b], tx_of(jnp.minimum(me + 1, last)))

        def ag_dn(l, c, b):
            return remote(yall.at[l, c, b], yall.at[l, c, b], ag_s.at[l, c, 1, b], ag_r.at[l, c, b], tx_of(jnp.maximum(me - 1, 0)))

        def gather_start(l, c):
            @pl.when(me < last)
            def _():
                ag_up(l, c, me).start()

            @pl.when(me > 0)
            def _():
                ag_dn(l, c, me).start()

        def gather_pass(l, c):
            for j in range(1, n_tx):
                @pl.when(me - j >= 0)
                def _():
                    ag_up(l, c, me - j).wait_recv()
                    @pl.when(me < last)
                    def _():
                        ag_up(l, c, me - j).start()

                @pl.when(me + j <= last)
                def _():
                    ag_dn(l, c, me + j).wait_recv()
                    @pl.when(me > 0)
                    def _():
                        ag_dn(l, c, me + j).start()

        def gather_end(l, c):
            for j in range(0, n_tx):
                @pl.when(jnp.logical_and(me - j >= 0, me < last))
                def _():
                    ag_up(l, c, me - j).wait_send()

                @pl.when(jnp.logical_and(me + j <= last, me > 0))
                def _():
                    ag_dn(l, c, me + j).wait_send()

        partner = ty_of(ty + 1 - 2 * core)
        across = ty_of(lax.rem(ty + 2, n_ty))
        mine = pl.ds(pl.multiple_of(core * half, half), half)
        other = pl.ds(pl.multiple_of((1 - core) * half, half), half)

        def s1_copy(l, q):
            return remote(s1o.at[l, q], s1i.at[l, q], s_s.at[l, 0, q], s_r.at[l, 0, q], partner)

        def s2_copy(l, q):
            return remote(s2o.at[l, q], s2i.at[l, q], s_s.at[l, 1, q], s_r.at[l, 1, q], across)

        def s3_copy(l, q):
            return remote(s3o.at[l, q], s3i.at[l, q], s_s.at[l, 2, q], s_r.at[l, 2, q], partner)

        row_i = lax.broadcasted_iota(jnp.int32, (128, 256), 0)
        col_i = lax.broadcasted_iota(jnp.int32, (128, 256), 1)
        pick = [(col_i == 2 * row_i + k).astype(F32).astype(BF16) for k in range(2)]

        outs = []

        def put(src, dst, sem):
            cp = pltpu.make_async_copy(src, dst, sem)
            cp.start()
            outs.append(cp)

        for l in range(n_layer):
            if l == 0:
                wait("r", "nw")
            sq = jnp.sum(r[...] * r[...], axis=-1, keepdims=True)
            sto[l] = jnp.broadcast_to(sq, (rows, 128)).T[0:8, :]
            if l == 0:
                pl.semaphore_wait(barrier, n_tx + n_ty - 2)
            for j in range(1, n_tx):
                stat_copy(l, lax.rem(me + j, n_tx)).start()
            sti[l, me] = sto[l]
            for j in range(1, n_tx):
                stat_recv(l, lax.rem(me + j, n_tx)).wait_recv()
            tot = sti[l, 0]
            for k in range(1, n_tx):
                tot = tot + sti[l, k]
            scale = lax.rsqrt(jnp.broadcast_to(tot[0:1, :], (128, rows)).T / d_model + NORM_EPS)
            for j in range(d_loc // 128):
                cols = pl.ds(j * 128, 128)
                h = (r[:, cols] * scale * nw[l : l + 1, cols]).astype(BF16)
                for k in range(2):
                    hx[k, :, pl.ds(j * 256, 256)] = dot(h, pick[k]).astype(BF16)

            def project(c):
                k, cc = c // n_c, c % n_c
                for t in range(0, chunk // 128, 2):
                    tile = cc * (chunk // 128) + t
                    if k == 0:
                        wait(("win", l, tile), ("win", l, tile + 1))
                    w = jnp.concatenate([win.at[l, tile + i].reshape(2 * d_loc, 128)[...] for i in range(2)], axis=1)
                    part = dot(hx[k], w).astype(BF16)
                    for b in range(n_tx):
                        own[l, c, b, :, pl.ds(t * 128, 256)] = part[b * blk : (b + 1) * blk, :]

            project(0)
            for c in range(1, n_c + 2):
                project(c)
                forward(l, c - 1)
            if l == 0:
                start(("wdt", 0), ("ss", 0), ("wout", 0))
                wait("cw", "cb", "db", "al", "ds", "cs")
            wait(("wx", l))
            p_part = jnp.zeros((blk, rank + 2 * n_state), F32)
            for c in range(n_c):
                cols = pl.ds(c * chunk, chunk)
                x_new = finish(l, c)
                xi[l, :, cols] = x_new
                val = x_new.astype(F32) * cw[l, 3:4, cols] + cb[l : l + 1, cols]
                for k in range(3):
                    val = val + cs[l, k, :, cols].astype(F32) * cw[l, k : k + 1, cols]
                x_act = (val * jax.nn.sigmoid(val)).astype(BF16)
                xc[:, cols] = x_act.astype(F32)
                p_part = p_part + lax.dot_general(x_act, wx[l, :, cols], (((1,), (1,)), ((), ())), preferred_element_type=F32)
            put(xi.at[l], conv_out.at[l, 2], out_sem.at[l, 0])
            put(cs.at[l, pl.ds(1, 2)], conv_out.at[l, pl.ds(0, 2)], out_sem.at[l, 1])
            pown[l] = p_part.astype(BF16)
            for j in range(1, n_ty):
                p_copy(l, lax.rem(ty + j, n_ty)).start()
            for c in range(n_c + 2, 2 * n_c):
                project(c)
                forward(l, c - 1)
            if l + 1 < n_layer:
                start(*[("win", l + 1, t) for t in range(n_w)])
                start(("wx", l + 1), ("wdt", l + 1), ("ss", l + 1), ("wout", l + 1))
            for j in range(1, n_ty):
                k = lax.rem(ty + j, n_ty)
                p_recv(l, k).wait_recv()
                p_part = p_part + pin[l, k].astype(F32)
            dt_low = p_part[:, :rank]
            dt_low = (dt_low * lax.rsqrt(jnp.mean(dt_low * dt_low, axis=-1, keepdims=True) + INNER_EPS)).astype(BF16)
            b_mat = p_part[:, rank : rank + n_state]
            b_mat = b_mat * lax.rsqrt(jnp.mean(b_mat * b_mat, axis=-1, keepdims=True) + INNER_EPS)
            c_mat = p_part[:, rank + n_state :]
            c_mat = c_mat * lax.rsqrt(jnp.mean(c_mat * c_mat, axis=-1, keepdims=True) + INNER_EPS)
            for i in range(2):
                mat_t = (b_mat, c_mat)[i].T
                for b in range(blk):
                    bc[i, b] = jnp.broadcast_to(mat_t[:, b : b + 1], (n_state, 128))
            forward(l, 2 * n_c - 1)
            wait(("wdt", l), ("ss", l))
            for c in range(n_c):
                cols = pl.ds(c * chunk, chunk)
                raw = dot(dt_low, wdt[l, :, cols]) + db[l : l + 1, cols]
                delta = jnp.maximum(raw, 0.0) + jnp.log1p(jnp.exp(-jnp.abs(raw)))
                dt[:, cols] = delta
                dx[:, cols] = delta * xc[:, cols]
                neg_a = -jnp.exp(al[l, :, cols]) * LOG2E

                def row_step(b, carry):
                    row = pl.ds(b, 1)
                    b_row = jnp.concatenate([bc[0, b]] * (chunk // 128), axis=1)
                    c_row = jnp.concatenate([bc[1, b]] * (chunk // 128), axis=1)
                    s_new = jnp.exp2(dt[row, cols] * neg_a) * ss[l, b, :, cols] + dx[row, cols] * b_row
                    ss[l, b, :, cols] = s_new
                    sv[row, cols] = jnp.sum(s_new * c_row, axis=0, keepdims=True)
                    return carry

                lax.fori_loop(0, blk, row_step, 0, unroll=4)
                put(ss.at[l, :, :, cols], ssm_out.at[l, :, :, cols], ssm_sem.at[l, c])
                z_new = finish(l, n_c + c).astype(F32)
                y = (sv[:, cols] + ds[l : l + 1, cols] * xc[:, cols]) * (z_new * jax.nn.sigmoid(z_new))
                yall[l, c, me] = y.astype(BF16)
                gather_start(l, c)
                if c > 0:
                    gather_pass(l, c - 1)
            wait(("wout", l))
            for c in range(n_c):
                if c == n_c - 1:
                    gather_pass(l, c)
                y_all = yall[l, c].reshape(rows, chunk)
                for q in range(n_q):
                    qc = pl.ds(q * qw, qw)
                    out = dot(y_all, wout[l, pl.ds(c * chunk, chunk), qc])
                    acc[:, qc] = out if c == 0 else acc[:, qc] + out
                    if c == n_c - 1:
                        s1o[l, q] = acc[other, qc].astype(BF16)
                        s1_copy(l, q).start()
            for q in range(n_q):
                s1_copy(l, q).wait_recv()
                s2o[l, q] = (acc[mine, pl.ds(q * qw, qw)] + s1i[l, q].astype(F32)).astype(BF16)
                s2_copy(l, q).start()
            for q in range(n_q):
                qc = pl.ds(q * qw, qw)
                s2_copy(l, q).wait_recv()
                tot = (s2o[l, q].astype(F32) + s2i[l, q].astype(F32)).astype(BF16)
                s3o[l, q] = tot
                s3_copy(l, q).start()
                r[mine, qc] += tot.astype(F32)
            for q in range(n_q):
                s3_copy(l, q).wait_recv()
                r[other, pl.ds(q * qw, qw)] += s3i[l, q].astype(F32)

        put(r, r_out, out_sem.at[0, 2])
        for l in range(n_layer):
            for c in range(2 * n_c):
                forward_end(l, c)
            for j in range(1, n_tx):
                stat_copy(l, lax.rem(me + j, n_tx)).wait_send()
            for j in range(1, n_ty):
                p_copy(l, lax.rem(ty + j, n_ty)).wait_send()
            for c in range(n_c):
                gather_end(l, c)
            for q in range(n_q):
                s1_copy(l, q).wait_send()
                s2_copy(l, q).wait_send()
                s3_copy(l, q).wait_send()
        for cp in outs:
            cp.wait()

    dma = lambda *s: pltpu.SemaphoreType.DMA(s)
    vm = lambda t, *s: pltpu.VMEM(s, t)
    nl = n_layer
    p_w = rank + 2 * n_state
    scratch = [
        vm(F32, rows, d_loc), vm(F32, nl, d_loc), vm(BF16, nl, n_w, d_loc, 2, 128), vm(F32, nl, 4, chan), vm(F32, nl, chan),
        vm(BF16, nl, p_w, chan), vm(BF16, nl, rank, chan), vm(F32, nl, chan), vm(F32, nl, n_state, chan), vm(F32, nl, chan),
        vm(BF16, nl, chan, d_loc), vm(BF16, nl, 3, blk, chan), vm(F32, nl, blk, n_state, chan),
        vm(BF16, 2, rows, 2 * d_loc), vm(BF16, nl, 2 * n_c, n_tx, blk, chunk), vm(BF16, nl, 2 * n_c, n_tx, blk, chunk), vm(BF16, nl, 2 * n_c, n_tx, blk, chunk),
        vm(F32, blk, chunk), vm(BF16, nl, blk, chan), vm(F32, blk, chan), vm(F32, blk, chan), vm(F32, blk, chan), vm(F32, blk, chan),
        vm(F32, 2, blk, n_state, 128), vm(BF16, nl, blk, p_w), vm(BF16, nl, n_ty, blk, p_w),
        vm(BF16, nl, n_c, n_tx, blk, chunk), vm(F32, rows, d_loc),
        *[vm(BF16, nl, n_q, half, qw) for _ in range(6)],
        vm(F32, nl, 8, 128), vm(F32, nl, n_tx, 8, 128),
        dma(8 + 4 * nl), dma(nl, n_w), dma(nl, 3), dma(nl, n_c),
        *[dma(nl, 2 * n_c, n_tx) for _ in range(4)],
        dma(nl, n_ty), dma(nl, n_ty), dma(nl, n_c, 2, n_tx), dma(nl, n_c, n_tx), dma(nl, 3, n_q), dma(nl, 3, n_q),
        dma(nl, n_tx), dma(nl, n_tx),
    ]
    return kernel, scratch


def solution(mesh):
    n_tx, n_ty = mesh.shape["tx"], mesh.shape["ty"]

    def local_step(residual, norm_w, w_in, conv_w, conv_b, w_x, w_dt, dt_bias, a_log, d_skip, w_out, conv_state, ssm_state):
        rows, d_loc = residual.shape
        n_layer, _, _, chan = w_in.shape
        rank, n_state = w_dt.shape[1], a_log.shape[-1]
        blk = rows // n_tx
        kernel, scratch = make_kernel(n_layer, n_tx, n_ty, rows, d_loc, chan, rank, n_state, 512)
        r_out, conv_out, ssm_out = pl.pallas_call(
            kernel,
            out_shape=(
                jax.ShapeDtypeStruct((rows, d_loc), F32),
                jax.ShapeDtypeStruct((n_layer, 3, blk, chan), BF16),
                jax.ShapeDtypeStruct((n_layer, blk, n_state, chan), F32),
            ),
            in_specs=[ANY] * 13,
            out_specs=(ANY, ANY, ANY),
            scratch_shapes=scratch,
            compiler_params=pltpu.CompilerParams(collective_id=0, has_side_effects=True, vmem_limit_bytes=67043328),
            name="mixer",
        )(
            residual, norm_w, w_in, conv_w.transpose(0, 2, 1), conv_b, w_x.transpose(0, 2, 1), w_dt, dt_bias,
            a_log.transpose(0, 2, 1), d_skip, w_out, conv_state.transpose(0, 3, 1, 2), ssm_state.transpose(0, 1, 3, 2),
        )
        return r_out, conv_out.transpose(0, 2, 3, 1), ssm_out.transpose(0, 1, 3, 2)

    cache_spec = P(None, ("dp", "tx"), "ty", None)
    in_specs = (P("dp", "tx"), P(None, "tx"), P(None, "tx", None, "ty"), P(None, "ty", None), P(None, "ty"), P(None, "ty", None), P(None, None, "ty"), P(None, "ty"), P(None, "ty", None), P(None, "ty"), P(None, "ty", "tx"), cache_spec, cache_spec)
    out_specs = (P("dp", "tx"), cache_spec, cache_spec)
    return jax.shard_map(local_step, mesh=mesh, in_specs=in_specs, out_specs=out_specs, check_vma=False)
```

time: 270 us -> 170 us (0.63)
  Pallas kernels: 0 us -> 157 us
  waiting for transfers between devices: 102 us -> 0 us
  blocking collectives: 78.5 us -> 0 us
  matrix products: 31.6 us -> 0 us
  other arithmetic: 27.1 us -> 0 us
  between operations: 14.2 us -> 0.65 us
  local copies, waits for them, and re-layouts: 16.3 us -> 11.9 us
    pallas_call x0 -> x1, Pallas kernels: none -> 157 us  [local_step(): pl.pallas_call(kernel, out_shape=(jax.ShapeDtypeStruct((rows, d_loc), F32...]
    psum x2 -> x0, waiting for transfers between devices: 51.8 us -> none  [sum_over_ty(): return lax.psum(part_sum.astype(jnp.bfloat16), 'ty').astype(jnp.float32)]
    reduce_scatter x2 -> x0, waiting for transfers between devices: 49.9 us -> none  [local_step(): lax.psum_scatter(proj_part.astype(jnp.bfloat16), 'tx', scatter_dimension=...]
    psum x4 -> x0, blocking collectives: 46.1 us -> none  [the longest x2 25.4 us: local_step(): sq_total = lax.psum(sq_part, 'tx')]
    all_gather x2 -> x0, blocking collectives: 32.5 us -> none  [local_step(): gated_rows = lax.all_gather(gated, 'tx', axis=0, tiled=True)]
    dot_general x8 -> x0, matrix products: 31.6 us -> none  [the longest x2 19.5 us: local_step(): jnp.einsum('bd,dke->bke', normed, w_in[layer_idx], preferred_element_type...]
    slice x5 -> x0, local copies, waits for them, and re-layouts: 14.4 us -> none  [the longest x1 14.3 us: local_step(): w_in[layer_idx]]
    unnamed x30 -> x3, local copies, waits for them, and re-layouts: 0.08 us -> 11.9 us
  transfers between devices with their start and end apart: 4 -> 0, of which waited for: 4 -> 0; matrix products, arithmetic and copies ran while one was open for 3% -> 0% of each run, Pallas kernels for 0% -> 0%
where the time goes in v1:
time: 170 us
  Pallas kernels  157 us (92%)
  local copies, waits for them, and re-layouts  11.9 us (7%)
    pallas_call x1, Pallas kernels, local_step(): pl.pallas_call(kernel, out_shape=(jax.ShapeDtypeStruct((rows, d_loc), F32...  157 us
    unnamed x3, local copies, waits for them, and re-layouts  11.9 us

profile of v1, /device:TPU:0, one launch (start us, length us, event | category | flops | bytes accessed | tf_op | source)
XLA Modules:
  0.0 169.9 jit_solution(13707307708039376744)
XLA Ops:
  0.6 157.4 %mixer.1 = (f32[128,1024]{1,0:T(8,128)}, bf16[2,3,32,2048]{3,2,1,0:T(8,128)(2,1)}, f32[2,32,16,2048]{3,2,1,0:T(8,128)}) custom-call(f32[128,1024]{1,0:T(8,128)} %r_hbm.1, f32[2,1024]{1,0:T(2,128)} %nw_hbm.1, bf16[2,1024,2,2048]{3,2,1,0:T(2,128)(2,1)} %win_hbm.1, f32[2,4,2048]{2,1,0:T(4,128)} %bitcast.13, f32[2,2048]{1,0:T(2,128)} %cb_hbm.1, ...), custom_call_target="tpu_custom_call" | custom-call | tf_op jit(solution)/shard_map/mixer/pallas_call | solution.py:379
  158.0 1.9 %copy.19 = f32[128,1024]{1,0:T(8,128)} copy(f32[128,1024]{1,0:T(8,128)} %get-tuple-element.12) | data formatting | bytes 1048576
  159.9 2.1 %copy.20 = bf16[2,32,2048,3]{2,1,3,0:T(8,128)(2,1)} copy(bf16[2,32,2048,3]{2,1,3,0:T(8,128)(2,1)} %bitcast.10) | data formatting | bytes 1572864
  162.0 7.9 %copy.21 = f32[2,32,2048,16]{2,3,1,0:T(8,128)} copy(f32[2,32,2048,16]{2,3,1,0:T(8,128)} %bitcast.7) | data formatting | bytes 16777216

commit v2 on v0

v2 whole, which is shorter than its diff:
```python
import jax
import jax.numpy as jnp
from jax import lax
from jax.experimental import pallas as pl
from jax.experimental.pallas import tpu as pltpu
from jax.sharding import PartitionSpec as P

NORM_EPS = 1e-5
INNER_EPS = 1e-6
LOG2E = 1.4426950408889634
BF16, F32 = jnp.bfloat16, jnp.float32
MESH = pl.DeviceIdType.MESH
ANY = pl.BlockSpec(memory_space=pl.ANY)
VMEM = pl.BlockSpec(memory_space=pltpu.VMEM)


def dot(a, b):
    return jnp.dot(a, b, preferred_element_type=F32)


def make_kernel(n_layer, n_tx, n_ty, rows, d_loc, chan, rank, n_state, chunk, n_g, n_q):
    blk = rows // n_tx
    hb = blk // n_g
    rg = n_tx * hb
    half = rg // 2
    n_c = chan // chunk
    d_model = d_loc * n_tx
    qw = d_loc // n_q
    n_w = chan // 128

    def kernel(
        r_hbm, nw_hbm, win_hbm, cw_hbm, cb_hbm, wx_hbm, wdt_hbm, db_hbm, al_hbm, ds_hbm, wout_hbm, cs_hbm, ss_hbm,
        r, xi, cs, ss,
        nw, win, cw, cb, wx, wdt, db, al, ds, wout,
        hx, own, cmb, fin, xc, dt, dx, sv, bc, pown, pin, yall, acc, s1o, s1i, s2o, s2i, s3o, s3i, sto, sti,
        ld_sem, r_sem, win_sem, rs_s, cm_r, fn_r, p_s, p_r, ag_s, ag_r, s_s, s_r, st_s, st_r,
    ):
        dp, me, ty = lax.axis_index("dp"), lax.axis_index("tx"), lax.axis_index("ty")
        core = lax.rem(ty, 2)
        mate = me + 1 - 2 * lax.rem(me, 2)
        mid = (me * (3 - me)) // 2
        o_end = 3 - me + mid * (me - mate)
        o_mid = 3 - mate + mid * (mate - me)
        barrier = pltpu.get_barrier_semaphore()

        def tx_of(k):
            return (dp, k, ty)

        def ty_of(k):
            return (dp, me, k)

        def remote(src, dst, ssem, rsem, dev):
            return pltpu.make_async_remote_copy(src_ref=src, dst_ref=dst, send_sem=ssem, recv_sem=rsem, device_id=dev, device_id_type=MESH)

        loads = {}
        for g in range(n_g):
            for b in range(n_tx):
                loads["r", g, b] = pltpu.make_async_copy(r_hbm.at[pl.ds(b * blk + g * hb, hb)], r.at[g, pl.ds(b * hb, hb)], r_sem.at[g, b])
        names = dict(nw=(nw_hbm, nw), cw=(cw_hbm, cw), cb=(cb_hbm, cb), db=(db_hbm, db), al=(al_hbm, al), ds=(ds_hbm, ds), cs=(cs_hbm, cs))
        for k, key in enumerate(names):
            loads[key] = pltpu.make_async_copy(names[key][0], names[key][1], ld_sem.at[k])
        for l in range(n_layer):
            for k, (key, src, dst) in enumerate((("wx", wx_hbm, wx), ("wdt", wdt_hbm, wdt), ("wout", wout_hbm, wout), ("ss", ss_hbm, ss))):
                loads[key, l] = pltpu.make_async_copy(src.at[l], dst.at[l], ld_sem.at[len(names) + 4 * l + k])
            for t in range(n_w):
                loads["win", l, t] = pltpu.make_async_copy(win_hbm.at[l, :, :, pl.ds(t * 128, 128)], win.at[l, t], win_sem.at[l, t])

        def start(*keys):
            for key in keys:
                loads[key].start()

        def wait(*keys):
            for key in keys:
                loads[key].wait()

        def stat_copy(l, g, k):
            return remote(sto.at[l, g], sti.at[l, g, me], st_s.at[l, g, k], st_r.at[l, g, me], tx_of(k))

        def stat_recv(l, g, k):
            return remote(sto.at[l, g], sti.at[l, g, k], st_s.at[l, g, k], st_r.at[l, g, k], tx_of(k))

        def to_mate(l, g, c):
            return remote(own.at[l, g, c, mate], fin.at[l, g, c, 0], rs_s.at[l, g, c, 2], fn_r.at[l, g, c, 0], tx_of(mate))

        def to_mid(l, g, c, k):
            return remote(own.at[l, g, c, (o_end, o_mid)[k]], cmb.at[l, g, c, k], rs_s.at[l, g, c, k], cm_r.at[l, g, c, k], tx_of(mate))

        def to_far(l, g, c, k):
            b = (o_end, o_mid)[k]
            return remote(own.at[l, g, c, b], fin.at[l, g, c, 1], rs_s.at[l, g, c, k], fn_r.at[l, g, c, 1], tx_of(b))

        def p_copy(l, g, k):
            return remote(pown.at[l, g], pin.at[l, g, ty], p_s.at[l, g, k], p_r.at[l, g, ty], ty_of(k))

        def p_recv(l, g, k):
            return remote(pown.at[l, g], pin.at[l, g, k], p_s.at[l, g, k], p_r.at[l, g, k], ty_of(k))

        def ag_copy(l, g, c, b, k, dev):
            return remote(yall.at[l, g, c, b], yall.at[l, g, c, b], ag_s.at[l, g, c, k], ag_r.at[l, g, c, b], tx_of(dev))

        partner = ty_of(ty + 1 - 2 * core)
        across = ty_of(lax.rem(ty + 2, n_ty))
        mine = pl.ds(pl.multiple_of(core * half, half), half)
        other = pl.ds(pl.multiple_of((1 - core) * half, half), half)

        def s_copy(i, l, g, q):
            src, dst = ((s1o, s1i), (s2o, s2i), (s3o, s3i))[i]
            return remote(src.at[l, g, q], dst.at[l, g, q], s_s.at[l, g, i, q], s_r.at[l, g, i, q], across if i == 1 else partner)

        def stat(l, g):
            sq = jnp.sum(r[g] * r[g], axis=-1, keepdims=True)
            sto[l, g] = jnp.broadcast_to(sq, (rg, 128)).T[0:8, :]

        def stat_send(l, g):
            for j in range(1, n_tx):
                stat_copy(l, g, lax.rem(me + j, n_tx)).start()
            sti[l, g, me] = sto[l, g]

        def head(l, g):
            for j in range(1, n_tx):
                stat_recv(l, g, lax.rem(me + j, n_tx)).wait_recv()
            tot = sti[l, g, 0]
            for k in range(1, n_tx):
                tot = tot + sti[l, g, k]
            scale = lax.rsqrt(jnp.broadcast_to(tot[0:1, :], (128, rg)).T / d_model + NORM_EPS)
            row_i = lax.broadcasted_iota(jnp.int32, (128, 256), 0)
            col_i = lax.broadcasted_iota(jnp.int32, (128, 256), 1)
            pick = [(col_i == 2 * row_i + k).astype(F32).astype(BF16) for k in range(2)]
            for j in range(d_loc // 128):
                cols = pl.ds(j * 128, 128)
                h = (r[g, :, cols] * scale * nw[l : l + 1, cols]).astype(BF16)
                for k in range(2):
                    hx[g, k * rg : (k + 1) * rg, pl.ds(j * 256, 256)] = dot(h, pick[k]).astype(BF16)

        def project(l, gs, c):
            lhs = hx[gs[0]] if len(gs) == 1 else hx[...].reshape(n_g * 2 * rg, 2 * d_loc)
            for t in range(0, chunk // 128, 2):
                tile = c * (chunk // 128) + t
                if gs[0] == 0:
                    wait(("win", l, tile), ("win", l, tile + 1))
                w = jnp.concatenate([win.at[l, tile + i].reshape(2 * d_loc, 128)[...] for i in range(2)], axis=1)
                part = dot(lhs, w).astype(BF16)
                for i, g in enumerate(gs):
                    for k in range(2):
                        for b in range(n_tx):
                            at = (2 * i + k) * rg + b * hb
                            own[l, g, k * n_c + c, b, :, pl.ds(t * 128, 256)] = part[at : at + hb, :]

        def send(l, g, c):
            @pl.when(mid == 0)
            def _():
                to_mid(l, g, c, 0).start()
                to_mid(l, g, c, 1).start()
            to_mate(l, g, c).start()

        def send_z(l, g):
            for c in range(n_c, 2 * n_c):
                send(l, g, c)

        def combine(l, g, c):
            @pl.when(mid == 1)
            def _():
                for k in range(2):
                    b = (o_end, o_mid)[k]
                    to_mid(l, g, c, k).wait_recv()
                    own[l, g, c, b] = (own[l, g, c, b].astype(F32) + cmb[l, g, c, k].astype(F32)).astype(BF16)
                    to_far(l, g, c, k).start()

        def finish(l, g, c):
            to_mate(l, g, c).wait_recv()
            to_far(l, g, c, 0).wait_recv()
            return (own[l, g, c, me].astype(F32) + fin[l, g, c, 0].astype(F32) + fin[l, g, c, 1].astype(F32)).astype(BF16)

        def x_phase(l, g):
            hrow = pl.ds(g * hb, hb)
            p_part = jnp.zeros((hb, rank + 2 * n_state), F32)
            for c in range(n_c):
                cols = pl.ds(c * chunk, chunk)
                x_new = finish(l, g, c)
                xi[l, hrow, cols] = x_new
                val = x_new.astype(F32) * cw[l, 3:4, cols] + cb[l : l + 1, cols]
                for k in range(3):
                    val = val + cs[l, k, hrow, cols].astype(F32) * cw[l, k : k + 1, cols]
                x_act = (val * jax.nn.sigmoid(val)).astype(BF16)
                xc[g, :, cols] = x_act.astype(F32)
                p_part = p_part + lax.dot_general(x_act, wx[l, :, cols], (((1,), (1,)), ((), ())), preferred_element_type=F32)
            pown[l, g] = p_part.astype(BF16)
            for j in range(1, n_ty):
                p_copy(l, g, lax.rem(ty + j, n_ty)).start()

        def d_phase(l, g):
            p_sum = pown[l, g].astype(F32)
            for j in range(1, n_ty):
                k = lax.rem(ty + j, n_ty)
                p_recv(l, g, k).wait_recv()
                p_sum = p_sum + pin[l, g, k].astype(F32)
            dt_low = p_sum[:, :rank]
            dt_low = (dt_low * lax.rsqrt(jnp.mean(dt_low * dt_low, axis=-1, keepdims=True) + INNER_EPS)).astype(BF16)
            for i in range(2):
                mat = p_sum[:, rank + i * n_state : rank + (i + 1) * n_state]
                mat_t = (mat * lax.rsqrt(jnp.mean(mat * mat, axis=-1, keepdims=True) + INNER_EPS)).T
                for b in range(hb):
                    bc[i, b] = jnp.broadcast_to(mat_t[:, b : b + 1], (n_state, 128))
            for c in range(n_c):
                cols = pl.ds(c * chunk, chunk)
                raw = dot(dt_low, wdt[l, :, cols]) + db[l : l + 1, cols]
                delta = jnp.maximum(raw, 0.0) + jnp.log1p(jnp.exp(-jnp.abs(raw)))
                dt[:, cols] = delta
                dx[:, cols] = delta * xc[g, :, cols]
                neg_a = -jnp.exp(al[l, :, cols]) * LOG2E

                def row_step(b, carry):
                    row = pl.ds(b, 1)
                    b_row = jnp.concatenate([bc[0, b]] * (chunk // 128), axis=1)
                    c_row = jnp.concatenate([bc[1, b]] * (chunk // 128), axis=1)
                    at = g * hb + b
                    s_new = jnp.exp2(dt[row, cols] * neg_a) * ss[l, at, :, cols] + dx[row, cols] * b_row
                    ss[l, at, :, cols] = s_new
                    sv[g, row, cols] = jnp.sum(s_new * c_row, axis=0, keepdims=True)
                    return carry

                lax.fori_loop(0, hb, row_step, 0, unroll=4)

        def y_phase(l, g, c):
            cols = pl.ds(c * chunk, chunk)
            z_new = finish(l, g, n_c + c).astype(F32)
            y = (sv[g, :, cols] + ds[l : l + 1, cols] * xc[g, :, cols]) * (z_new * jax.nn.sigmoid(z_new))
            yall[l, g, c, me] = y.astype(BF16)
            ag_copy(l, g, c, me, 0, mate).start()

            @pl.when(mid == 1)
            def _():
                ag_copy(l, g, c, me, 1, 3 - me).start()

        def gather_1(l, g, c):
            ag_copy(l, g, c, mate, 0, mate).wait_recv()

            @pl.when(mid == 1)
            def _():
                ag_copy(l, g, c, mate, 2, 3 - me).start()

        def gather_2(l, g, c):
            ag_copy(l, g, c, o_mid, 0, mate).wait_recv()

            @pl.when(mid == 1)
            def _():
                ag_copy(l, g, c, o_mid, 3, mate).start()

            ag_copy(l, g, c, o_end, 0, mate).wait_recv()

            @pl.when(mid == 1)
            def _():
                ag_copy(l, g, c, o_end, 4, mate).start()

        def w_phase(l, g, c):
            y_all = yall[l, g, c].reshape(rg, chunk)
            for q in range(n_q):
                qc = pl.ds(q * qw, qw)
                out = dot(y_all, wout[l, pl.ds(c * chunk, chunk), qc])
                acc[g, :, qc] = out if c == 0 else acc[g, :, qc] + out
                if c == n_c - 1:
                    s1o[l, g, q] = acc[g, other, qc].astype(BF16)
                    s_copy(0, l, g, q).start()

        def sum_1(l, g):
            for q in range(n_q):
                s_copy(0, l, g, q).wait_recv()
                s2o[l, g, q] = (acc[g, mine, pl.ds(q * qw, qw)] + s1i[l, g, q].astype(F32)).astype(BF16)
                s_copy(1, l, g, q).start()

        def sum_2(l, g):
            for q in range(n_q):
                qc = pl.ds(q * qw, qw)
                s_copy(1, l, g, q).wait_recv()
                tot = (s2o[l, g, q].astype(F32) + s2i[l, g, q].astype(F32)).astype(BF16)
                s3o[l, g, q] = tot
                s_copy(2, l, g, q).start()
                r[g, mine, qc] += tot.astype(F32)

        def sum_3(l, g):
            for q in range(n_q):
                s_copy(2, l, g, q).wait_recv()
                r[g, other, pl.ds(q * qw, qw)] += s3i[l, g, q].astype(F32)

        ph = dict(
            stat=stat, stat_send=stat_send, head=head, send=send, send_z=send_z, combine=combine, x=x_phase, d=d_phase,
            y=y_phase, g1=gather_1, g2=gather_2, w=w_phase, s1=sum_1, s2=sum_2, s3=sum_3,
        )

        def run(name, *args):
            with jax.named_scope(name + "_" + "_".join(map(str, args))):
                ph[name](*args)

        def proj(l, gs, c):
            with jax.named_scope(f"proj_{l}_{gs[0]}_{c}"):
                project(l, gs, c)
            for g in gs:
                send(l, g, c)

        groups = range(n_g)
        for g in groups:
            start(*[("r", g, b) for b in range(n_tx)])
        start("nw", *[("win", 0, t) for t in range(n_w)])
        for k in range(1, n_tx):
            pl.semaphore_signal(barrier, 1, device_id=tx_of(lax.rem(me + k, n_tx)), device_id_type=MESH)
        for k in range(1, n_ty):
            pl.semaphore_signal(barrier, 1, device_id=ty_of(lax.rem(ty + k, n_ty)), device_id_type=MESH)
        for g in groups:
            wait(*[("r", g, b) for b in range(n_tx)])
            run("stat", 0, g)
        pl.semaphore_wait(barrier, n_tx + n_ty - 2)
        for g in groups:
            run("stat_send", 0, g)
        start("cw", "cb", "db", "al", "ds", "cs", ("wx", 0), ("wdt", 0), ("ss", 0), ("wout", 0))
        wait("nw")
        for l in range(n_layer):
            if l == 0:
                for g in groups:
                    run("head", l, g)
                for c in range(n_c):
                    proj(l, (0, 1), c)
                    if c > 1:
                        run("combine", l, 0, c - 2)
                        run("combine", l, 1, c - 2)
                start(*[("win", 1, t) for t in range(n_w)])
                start(("wx", 1), ("wdt", 1), ("ss", 1), ("wout", 1))
                wait("cw", "cb", "db", "al", "ds", "cs", ("wx", 0))
                run("send_z", l, 0)
                run("send_z", l, 1)
                for c in (n_c - 2, n_c - 1):
                    run("combine", l, 0, c)
                for c in (n_c - 2, n_c - 1):
                    run("combine", l, 1, c)
            else:
                run("head", l, 0)
                proj(l, (0,), 0)
                proj(l, (0,), 1)
                run("s1", l - 1, 1)
                run("combine", l, 0, 0)
                proj(l, (0,), 2)
                run("combine", l, 0, 1)
                proj(l, (0,), 3)
                run("send_z", l, 0)
                run("s2", l - 1, 1)
                run("combine", l, 0, 2)
                run("s3", l - 1, 1)
                run("stat", l, 1)
                run("stat_send", l, 1)
                run("combine", l, 0, 3)
                wait(("wx", l))
            run("x", l, 0)
            if l > 0:
                run("head", l, 1)
                for c in range(n_c):
                    proj(l, (1,), c)
                    run("combine", l, 0, n_c + c)
                    if c > 1:
                        run("combine", l, 1, c - 2)
                run("send_z", l, 1)
            else:
                for c in range(n_c):
                    run("combine", l, 0, n_c + c)
            if l == 0:
                run("x", l, 1)
            wait(("wdt", l), ("ss", l))
            run("d", l, 0)
            for c in range(n_c):
                run("y", l, 0, c)
            if l > 0:
                run("combine", l, 1, n_c - 2)
                run("combine", l, 1, n_c - 1)
                for c in range(n_c):
                    run("g1", l, 0, c)
                run("x", l, 1)
            else:
                for c in range(n_c):
                    run("g1", l, 0, c)
            for c in range(n_c):
                run("combine", l, 1, n_c + c)
            wait(("wout", l))
            for c in range(n_c):
                run("g2", l, 0, c)
                run("w", l, 0, c)
            run("d", l, 1)
            run("s1", l, 0)
            for c in range(n_c):
                run("y", l, 1, c)
            run("s2", l, 0)
            run("s3", l, 0)
            if l + 1 < n_layer:
                run("stat", l + 1, 0)
                run("stat_send", l + 1, 0)
            for c in range(n_c):
                run("g1", l, 1, c)
            for c in range(n_c):
                run("g2", l, 1, c)
                run("w", l, 1, c)
        run("s1", n_layer - 1, 1)
        run("s2", n_layer - 1, 1)
        run("s3", n_layer - 1, 1)

        for l in range(n_layer):
            for g in groups:
                for j in range(1, n_tx):
                    stat_copy(l, g, lax.rem(me + j, n_tx)).wait_send()
                for c in range(2 * n_c):
                    to_mate(l, g, c).wait_send()
                    to_mid(l, g, c, 0).wait_send()
                    to_mid(l, g, c, 1).wait_send()
                for j in range(1, n_ty):
                    p_copy(l, g, lax.rem(ty + j, n_ty)).wait_send()
                for c in range(n_c):
                    ag_copy(l, g, c, me, 0, mate).wait_send()

                    @pl.when(mid == 1)
                    def _():
                        for k in range(1, 5):
                            ag_copy(l, g, c, me, k, mate).wait_send()
                for q in range(n_q):
                    for i in range(3):
                        s_copy(i, l, g, q).wait_send()

    def dma(*s):
        return pltpu.SemaphoreType.DMA(s)

    def vm(t, *s):
        return pltpu.VMEM(s, t)

    nl, p_w = n_layer, rank + 2 * n_state
    scratch = [
        vm(F32, nl, d_loc), vm(BF16, nl, n_w, d_loc, 2, 128), vm(F32, nl, 4, chan), vm(F32, nl, chan),
        vm(BF16, nl, p_w, chan), vm(BF16, nl, rank, chan), vm(F32, nl, chan), vm(F32, nl, n_state, chan), vm(F32, nl, chan),
        vm(BF16, nl, chan, d_loc),
        vm(BF16, n_g, 2 * rg, 2 * d_loc), vm(BF16, nl, n_g, 2 * n_c, n_tx, hb, chunk),
        vm(BF16, nl, n_g, 2 * n_c, 2, hb, chunk), vm(BF16, nl, n_g, 2 * n_c, 2, hb, chunk),
        vm(F32, n_g, hb, chan), vm(F32, hb, chan), vm(F32, hb, chan), vm(F32, n_g, hb, chan),
        vm(F32, 2, hb, n_state, 128), vm(BF16, nl, n_g, hb, p_w), vm(BF16, nl, n_g, n_ty, hb, p_w),
        vm(BF16, nl, n_g, n_c, n_tx, hb, chunk), vm(F32, n_g, rg, d_loc),
        *[vm(BF16, nl, n_g, n_q, half, qw) for _ in range(6)],
        vm(F32, nl, n_g, 8, rg), vm(F32, nl, n_g, n_tx, 8, rg),
        dma(7 + 4 * nl), dma(n_g, n_tx), dma(nl, n_w),
        dma(nl, n_g, 2 * n_c, 3), dma(nl, n_g, 2 * n_c, 2), dma(nl, n_g, 2 * n_c, 2),
        dma(nl, n_g, n_ty), dma(nl, n_g, n_ty), dma(nl, n_g, n_c, 5), dma(nl, n_g, n_c, n_tx),
        dma(nl, n_g, 3, n_q), dma(nl, n_g, 3, n_q), dma(nl, n_g, n_tx), dma(nl, n_g, n_tx),
    ]
    outs = (vm(F32, n_g, rg, d_loc), vm(BF16, nl, blk, chan), vm(BF16, nl, 3, blk, chan), vm(F32, nl, blk, n_state, chan))
    return kernel, outs, scratch


def store_kernel(r, xi, cs, ss, r_out, conv_out, ssm_out, sem):
    n_g, rg, _ = r.shape
    nl, blk = ss.shape[:2]
    hb = blk // n_g
    pairs = []
    for l in range(nl):
        for i in range(0, blk, 8):
            pairs.append((ss.at[l, pl.ds(i, 8)], ssm_out.at[l, pl.ds(i, 8)]))
    for l in range(nl):
        pairs.append((cs.at[l, pl.ds(1, 2)], conv_out.at[l, pl.ds(0, 2)]))
        pairs.append((xi.at[l], conv_out.at[l, 2]))
    for g in range(n_g):
        for b in range(rg // hb):
            pairs.append((r.at[g, pl.ds(b * hb, hb)], r_out.at[pl.ds(b * blk + g * hb, hb)]))
    copies = [pltpu.make_async_copy(src, dst, sem.at[i]) for i, (src, dst) in enumerate(pairs)]
    for cp in copies:
        cp.start()
    for cp in copies:
        cp.wait()


def solution(mesh):
    n_tx, n_ty = mesh.shape["tx"], mesh.shape["ty"]

    def local_step(residual, norm_w, w_in, conv_w, conv_b, w_x, w_dt, dt_bias, a_log, d_skip, w_out, conv_state, ssm_state):
        rows, d_loc = residual.shape
        n_layer, _, _, chan = w_in.shape
        rank, n_state = w_dt.shape[1], a_log.shape[-1]
        blk = rows // n_tx
        kernel, outs, scratch = make_kernel(n_layer, n_tx, n_ty, rows, d_loc, chan, rank, n_state, 512, 2, 2)
        parts = pl.pallas_call(
            kernel,
            out_shape=outs,
            in_specs=[ANY] * 13,
            out_specs=(VMEM,) * 4,
            scratch_shapes=scratch,
            compiler_params=pltpu.CompilerParams(collective_id=0, has_side_effects=True, vmem_limit_bytes=67043328 - 11 * 2**20),
            name="mixer",
        )(
            residual, norm_w, w_in, conv_w.transpose(0, 2, 1), conv_b, w_x.transpose(0, 2, 1), w_dt, dt_bias,
            a_log.transpose(0, 2, 1), d_skip, w_out, conv_state.transpose(0, 3, 1, 2), ssm_state.transpose(0, 1, 3, 2),
        )
        r_out, conv_out, ssm_out = pl.pallas_call(
            store_kernel,
            out_shape=(
                jax.ShapeDtypeStruct((rows, d_loc), F32),
                jax.ShapeDtypeStruct((n_layer, 3, blk, chan), BF16),
                jax.ShapeDtypeStruct((n_layer, blk, n_state, chan), F32),
            ),
            in_specs=[VMEM] * 4,
            out_specs=(ANY,) * 3,
            scratch_shapes=[pltpu.SemaphoreType.DMA((64,))],
            compiler_params=pltpu.CompilerParams(vmem_limit_bytes=12 * 2**20),
            name="store",
        )(*parts)
        return r_out, conv_out.transpose(0, 2, 3, 1), ssm_out.transpose(0, 1, 3, 2)

    cache_spec = P(None, ("dp", "tx"), "ty", None)
    in_specs = (P("dp", "tx"), P(None, "tx"), P(None, "tx", None, "ty"), P(None, "ty", None), P(None, "ty"), P(None, "ty", None), P(None, None, "ty"), P(None, "ty"), P(None, "ty", None), P(None, "ty"), P(None, "ty", "tx"), cache_spec, cache_spec)
    out_specs = (P("dp", "tx"), cache_spec, cache_spec)
    return jax.shard_map(local_step, mesh=mesh, in_specs=in_specs, out_specs=out_specs, check_vma=False)
```

time: 270 us -> 111 us (0.41)
  Pallas kernels: 0 us -> 111 us
  waiting for transfers between devices: 102 us -> 0 us
  blocking collectives: 78.5 us -> 0 us
  matrix products: 31.6 us -> 0 us
  other arithmetic: 27.1 us -> 0 us
  local copies, waits for them, and re-layouts: 16.3 us -> 0 us
  between operations: 14.2 us -> 0.82 us
    pallas_call x0 -> x2, Pallas kernels: none -> 111 us  [the longest x1 106 us: local_step(): pl.pallas_call(kernel, out_shape=outs, in_specs=[ANY] * 13, out_specs=(VM...]
    psum x2 -> x0, waiting for transfers between devices: 51.8 us -> none  [sum_over_ty(): return lax.psum(part_sum.astype(jnp.bfloat16), 'ty').astype(jnp.float32)]
    reduce_scatter x2 -> x0, waiting for transfers between devices: 49.9 us -> none  [local_step(): lax.psum_scatter(proj_part.astype(jnp.bfloat16), 'tx', scatter_dimension=...]
    psum x4 -> x0, blocking collectives: 46.1 us -> none  [the longest x2 25.4 us: local_step(): sq_total = lax.psum(sq_part, 'tx')]
    all_gather x2 -> x0, blocking collectives: 32.5 us -> none  [local_step(): gated_rows = lax.all_gather(gated, 'tx', axis=0, tiled=True)]
    dot_general x8 -> x0, matrix products: 31.6 us -> none  [the longest x2 19.5 us: local_step(): jnp.einsum('bd,dke->bke', normed, w_in[layer_idx], preferred_element_type...]
    slice x5 -> x0, local copies, waits for them, and re-layouts: 14.4 us -> none  [the longest x1 14.3 us: local_step(): w_in[layer_idx]]
    add x2 -> x0, other arithmetic: 10.1 us -> none  [the longest x1 8.27 us: channel_update(): decay * ssm_prev + (delta * x_float)[:, :, None] * b_mat[:, None, :]]
  transfers between devices with their start and end apart: 4 -> 0, of which waited for: 4 -> 0; matrix products, arithmetic and copies ran while one was open for 3% -> 0% of each run, Pallas kernels for 0% -> 0%
where the time goes in v2:
time: 111 us
  Pallas kernels  111 us (100%)
    pallas_call x1, Pallas kernels, local_step(): pl.pallas_call(kernel, out_shape=outs, in_specs=[ANY] * 13, out_specs=(VM...  106 us
    pallas_call x1, Pallas kernels, local_step(): pl.pallas_call(store_kernel, out_shape=(jax.ShapeDtypeStruct((rows, d_loc...  4.22 us

profile of v2, /device:TPU:0, one launch (start us, length us, event | category | flops | bytes accessed | tf_op | source)
XLA Modules:
  0.0 111.3 jit_solution(12740236789949801272)
XLA Ops:
  0.6 106.3 %mixer.1 = (f32[2,64,1024]{2,1,0:T(8,128)S(1)}, bf16[2,32,2048]{2,1,0:T(8,128)(2,1)S(1)}, bf16[2,3,32,2048]{3,2,1,0:T(8,128)(2,1)S(1)}, f32[2,32,16,2048]{3,2,1,0:T(8,128)S(1)}) custom-call(f32[128,1024]{1,0:T(8,128)} %r_hbm.1, f32[2,1024]{1,0:T(2,128)} %nw_hbm.1, bf16[2,1024,2,2048]{3,2,1,0:T(2,128)(2,1)} %win_hbm.1, f32[2,4,2048]{2,1,0:T(4,128)} %bitcast.11, ...), custom_call_target="tpu_custom_call" | custom-call | tf_op jit(solution)/shard_map/mixer/pallas_call | solution.py:480
  106.9 4.2 %store.1 = (f32[128,1024]{1,0:T(8,128)}, bf16[2,3,32,2048]{3,2,1,0:T(8,128)(2,1)}, f32[2,32,16,2048]{3,2,1,0:T(8,128)}) custom-call(f32[2,64,1024]{2,1,0:T(8,128)S(1)} %get-tuple-element.10.r, bf16[2,32,2048]{2,1,0:T(8,128)(2,1)S(1)} %get-tuple-element.11.xi, bf16[2,3,32,2048]{3,2,1,0:T(8,128)(2,1)S(1)} %get-tuple-element.12.cs, ...), custom_call_target="tpu_custom_call" | custom-call | tf_op jit(solution)/shard_map/store/pallas_call | solution.py:492

commit v3 on v2

v3 whole, which is shorter than its diff:
```python
import jax
import jax.numpy as jnp
from jax import lax
from jax.experimental import pallas as pl
from jax.experimental.pallas import tpu as pltpu
from jax.sharding import PartitionSpec as P

NORM_EPS = 1e-5
INNER_EPS = 1e-6
LOG2E = 1.4426950408889634
BF16, F32 = jnp.bfloat16, jnp.float32
MESH = pl.DeviceIdType.MESH
ANY = pl.BlockSpec(memory_space=pl.ANY)
VMEM = pl.BlockSpec(memory_space=pltpu.VMEM)


def dot(a, b):
    return jnp.dot(a, b, preferred_element_type=F32)


def make_kernel(n_layer, n_tx, n_ty, rows, d_loc, chan, rank, n_state, chunk, n_g, n_q):
    blk = rows // n_tx
    hb = blk // n_g
    rg = n_tx * hb
    half = rg // 2
    n_c = chan // chunk
    d_model = d_loc * n_tx
    qw = d_loc // n_q
    n_w = chan // 128

    def kernel(
        r_hbm, nw_hbm, win_hbm, cw_hbm, cb_hbm, wx_hbm, wdt_hbm, db_hbm, al_hbm, ds_hbm, wout_hbm, cs_hbm, ss_hbm,
        r, xi, cs, ss,
        nw, win, cw, cb, wx, wdt, db, al, ds, wout,
        hx, own, cmb, fin, xc, dt, dx, sv, bc, pown, pin, yall, acc, so, si, sto, sti, sc,
        ld_sem, r_sem, win_sem, rs_s, cm_r, fn_r, p_s, p_r, ag_s, ag_r, s_s, s_r, st_s, st_r,
    ):
        dp, me, ty = lax.axis_index("dp"), lax.axis_index("tx"), lax.axis_index("ty")
        core = lax.rem(ty, 2)
        mate = me + 1 - 2 * lax.rem(me, 2)
        mid = (me * (3 - me)) // 2
        o_end = 3 - me + mid * (me - mate)
        o_mid = 3 - mate + mid * (mate - me)
        lo = 2 * (1 - me // 2)
        barrier = pltpu.get_barrier_semaphore()

        def tx_of(k):
            return (dp, k, ty)

        def ty_of(k):
            return (dp, me, k)

        def remote(src, dst, ssem, rsem, dev):
            return pltpu.make_async_remote_copy(src_ref=src, dst_ref=dst, send_sem=ssem, recv_sem=rsem, device_id=dev, device_id_type=MESH)

        loads = {}
        for g in range(n_g):
            for b in range(n_tx):
                loads["r", g, b] = pltpu.make_async_copy(r_hbm.at[pl.ds(b * blk + g * hb, hb)], r.at[g, pl.ds(b * hb, hb)], r_sem.at[g, b])
        names = dict(nw=(nw_hbm, nw), cw=(cw_hbm, cw), cb=(cb_hbm, cb), db=(db_hbm, db), al=(al_hbm, al), ds=(ds_hbm, ds), cs=(cs_hbm, cs))
        for k, key in enumerate(names):
            loads[key] = pltpu.make_async_copy(names[key][0], names[key][1], ld_sem.at[k])
        for l in range(n_layer):
            for k, (key, src, dst) in enumerate((("wx", wx_hbm, wx), ("wdt", wdt_hbm, wdt), ("wout", wout_hbm, wout), ("ss", ss_hbm, ss))):
                loads[key, l] = pltpu.make_async_copy(src.at[l], dst.at[l], ld_sem.at[len(names) + 4 * l + k])
            for t in range(n_w):
                loads["win", l, t] = pltpu.make_async_copy(win_hbm.at[l, :, :, pl.ds(t * 128, 128)], win.at[l, t], win_sem.at[l, t])

        def start(*keys):
            for key in keys:
                loads[key].start()

        def wait(*keys):
            for key in keys:
                loads[key].wait()

        partner_ty = ty + 1 - 2 * core
        partner = ty_of(partner_ty)
        across = ty_of(lax.rem(ty + 2, n_ty))
        mine = pl.ds(pl.multiple_of(core * half, half), half)
        other = pl.ds(pl.multiple_of((1 - core) * half, half), half)

        def stat_copy(l, g, j, rel):
            dev = (dp, lax.rem(me + j, n_tx), partner_ty if rel else ty)
            return remote(sto.at[l, g], sti.at[l, g, 2 * j + rel - 1], st_s, st_r.at[l, g], dev)

        def to_mate(l, g, c):
            return remote(own.at[l, g, c, mate], fin.at[l, g, c, 0], rs_s, fn_r.at[l, g, c], tx_of(mate))

        def to_mid(l, g, c):
            return remote(own.at[l, g, c, pl.ds(lo, 2)], cmb.at[l, g, c], rs_s, cm_r.at[l, g, c], tx_of(mate))

        def to_far(l, g, c, k):
            b = (o_end, o_mid)[k]
            return remote(own.at[l, g, c, b], fin.at[l, g, c, 1], rs_s, fn_r.at[l, g, c], tx_of(b))

        def p_copy(l, g, j):
            return remote(pown.at[l, g], pin.at[l, g, j - 1], p_s, p_r.at[l, g], ty_of(lax.rem(ty + j, n_ty)))

        def ag_copy(l, g, c, b, k, dev):
            return remote(yall.at[l, g, c, b], yall.at[l, g, c, b], ag_s, ag_r.at[l, g, c, k], tx_of(dev))

        def s_copy(i, l, g, q):
            return remote(so.at[i, l, g, q], si.at[i, l, g, q], s_s, s_r.at[l, g, i, q], across if i == 1 else partner)

        def all_of(ref, ssem, rsem):
            return remote(ref, ref, ssem, rsem, partner)

        def stat(l, g):
            part = r[g, mine, :]
            sq = jnp.sum(part * part, axis=-1, keepdims=True)
            sto[l, g] = jnp.broadcast_to(sq, (half, 128)).T[0:8, :]
            for j in range(n_tx - 1, -1, -1):
                for rel in range(2):
                    if j or rel:
                        stat_copy(l, g, j, rel).start()

        def head(l, g):
            all_of(sti.at[l, g], st_s, st_r.at[l, g]).wait_recv()
            for rel, at in enumerate((mine, other)):
                tot = sto[l, g] if rel == 0 else sti[l, g, 0]
                for j in range(1, n_tx):
                    tot = tot + sti[l, g, 2 * j + rel - 1]
                sc[at, :] = lax.rsqrt(jnp.broadcast_to(tot[0:1, :], (128, half)).T / d_model + NORM_EPS)
            scale = sc[...]
            row_i = lax.broadcasted_iota(jnp.int32, (128, 256), 0)
            col_i = lax.broadcasted_iota(jnp.int32, (128, 256), 1)
            pick = [(col_i == 2 * row_i + k).astype(F32).astype(BF16) for k in range(2)]
            for j in range(d_loc // 128):
                cols = pl.ds(j * 128, 128)
                h = (r[g, :, cols] * scale * nw[l : l + 1, cols]).astype(BF16)
                for k in range(2):
                    hx[g, k * rg : (k + 1) * rg, pl.ds(j * 256, 256)] = dot(h, pick[k]).astype(BF16)

        def project(l, gs, c):
            lhs = hx[gs[0]] if len(gs) == 1 else hx[...].reshape(n_g * 2 * rg, 2 * d_loc)
            for t in range(0, chunk // 128, 2):
                tile = c * (chunk // 128) + t
                if gs[0] == 0:
                    wait(("win", l, tile), ("win", l, tile + 1))
                w = jnp.concatenate([win.at[l, tile + i].reshape(2 * d_loc, 128)[...] for i in range(2)], axis=1)
                part = dot(lhs, w).astype(BF16)
                for i, g in enumerate(gs):
                    for k in range(2):
                        for b in range(n_tx):
                            at = (2 * i + k) * rg + b * hb
                            own[l, g, k * n_c + c, b, :, pl.ds(t * 128, 256)] = part[at : at + hb, :]

        def send(l, g, c):
            @pl.when(mid == 0)
            def _():
                to_mid(l, g, c).start()
            to_mate(l, g, c).start()

        def combine(l, g, c):
            @pl.when(mid == 1)
            def _():
                to_mid(l, g, c).wait_recv()
                for k in range(2):
                    b = (o_end, o_mid)[k]
                    own[l, g, c, b] = (own[l, g, c, b].astype(F32) + cmb[l, g, c, b - lo].astype(F32)).astype(BF16)
                    to_far(l, g, c, k).start()

        def finish(l, g, c):
            all_of(fin.at[l, g, c], rs_s, fn_r.at[l, g, c]).wait_recv()
            return (own[l, g, c, me].astype(F32) + fin[l, g, c, 0].astype(F32) + fin[l, g, c, 1].astype(F32)).astype(BF16)

        def x_phase(l, g):
            hrow = pl.ds(g * hb, hb)
            p_part = jnp.zeros((hb, rank + 2 * n_state), F32)
            for c in range(n_c):
                cols = pl.ds(c * chunk, chunk)
                x_new = finish(l, g, c)
                xi[l, hrow, cols] = x_new
                val = x_new.astype(F32) * cw[l, 3:4, cols] + cb[l : l + 1, cols]
                for k in range(3):
                    val = val + cs[l, k, hrow, cols].astype(F32) * cw[l, k : k + 1, cols]
                x_act = (val * jax.nn.sigmoid(val)).astype(BF16)
                xc[g, :, cols] = x_act.astype(F32)
                p_part = p_part + lax.dot_general(x_act, wx[l, :, cols], (((1,), (1,)), ((), ())), preferred_element_type=F32)
            pown[l, g] = p_part.astype(BF16)
            for j in range(1, n_ty):
                p_copy(l, g, j).start()

        def d_phase(l, g):
            p_sum = pown[l, g].astype(F32)
            all_of(pin.at[l, g], p_s, p_r.at[l, g]).wait_recv()
            for j in range(n_ty - 1):
                p_sum = p_sum + pin[l, g, j].astype(F32)
            dt_low = p_sum[:, :rank]
            dt_low = (dt_low * lax.rsqrt(jnp.mean(dt_low * dt_low, axis=-1, keepdims=True) + INNER_EPS)).astype(BF16)
            for i in range(2):
                mat = p_sum[:, rank + i * n_state : rank + (i + 1) * n_state]
                mat_t = (mat * lax.rsqrt(jnp.mean(mat * mat, axis=-1, keepdims=True) + INNER_EPS)).T
                for b in range(hb):
                    bc[i, b] = jnp.broadcast_to(mat_t[:, b : b + 1], (n_state, 128))
            for c in range(n_c):
                cols = pl.ds(c * chunk, chunk)
                raw = dot(dt_low, wdt[l, :, cols]) + db[l : l + 1, cols]
                delta = jnp.maximum(raw, 0.0) + jnp.log1p(jnp.exp(-jnp.abs(raw)))
                dt[:, cols] = delta
                dx[:, cols] = delta * xc[g, :, cols]
                neg_a = al[l, :, cols]

                def row_step(b, carry):
                    row = pl.ds(b, 1)
                    b_row = jnp.concatenate([bc[0, b]] * (chunk // 128), axis=1)
                    c_row = jnp.concatenate([bc[1, b]] * (chunk // 128), axis=1)
                    at = g * hb + b
                    s_new = jnp.exp2(dt[row, cols] * neg_a) * ss[l, at, :, cols] + dx[row, cols] * b_row
                    ss[l, at, :, cols] = s_new
                    sv[g, row, cols] = jnp.sum(s_new * c_row, axis=0, keepdims=True)
                    return carry

                lax.fori_loop(0, hb, row_step, 0, unroll=4)

        def y_phase(l, g, c):
            cols = pl.ds(c * chunk, chunk)
            z_new = finish(l, g, n_c + c).astype(F32)
            y = (sv[g, :, cols] + ds[l : l + 1, cols] * xc[g, :, cols]) * (z_new * jax.nn.sigmoid(z_new))
            yall[l, g, c, me] = y.astype(BF16)

            @pl.when(mid == 0)
            def _():
                ag_copy(l, g, c, me, 0, o_mid).start()

            ag_copy(l, g, c, me, 1, mate).start()

            @pl.when(mid == 1)
            def _():
                ag_copy(l, g, c, me, 1, o_end).start()
                ag_copy(l, g, c, me, 1, o_mid).start()

        def gather(l, g, c):
            @pl.when(mid == 1)
            def _():
                ag_copy(l, g, c, o_end, 0, mate).wait_recv()
                ag_copy(l, g, c, o_end, 0, mate).start()

        def w_phase(l, g, c):
            @pl.when(mid == 0)
            def _():
                ag_copy(l, g, c, o_end, 0, mate).wait_recv()
            all_of(yall.at[l, g, c, pl.ds(0, 2)], ag_s, ag_r.at[l, g, c, 1]).wait_recv()
            y_all = yall[l, g, c].reshape(rg, chunk)
            for q in range(n_q):
                qc = pl.ds(q * qw, qw)
                out = dot(y_all, wout[l, pl.ds(c * chunk, chunk), qc])
                acc[g, :, qc] = out if c == 0 else acc[g, :, qc] + out
                if c == n_c - 1:
                    so[0, l, g, q] = acc[g, other, qc].astype(BF16)
                    s_copy(0, l, g, q).start()

        def sum_1(l, g):
            for q in range(n_q):
                s_copy(0, l, g, q).wait_recv()
                so[1, l, g, q] = (acc[g, mine, pl.ds(q * qw, qw)] + si[0, l, g, q].astype(F32)).astype(BF16)
                s_copy(1, l, g, q).start()

        def sum_2(l, g):
            for q in range(n_q):
                qc = pl.ds(q * qw, qw)
                s_copy(1, l, g, q).wait_recv()
                tot = (so[1, l, g, q].astype(F32) + si[1, l, g, q].astype(F32)).astype(BF16)
                so[2, l, g, q] = tot
                s_copy(2, l, g, q).start()
                r[g, mine, qc] += tot.astype(F32)

        def sum_3(l, g):
            for q in range(n_q):
                s_copy(2, l, g, q).wait_recv()
                r[g, other, pl.ds(q * qw, qw)] += si[2, l, g, q].astype(F32)

        ph = dict(
            stat=stat, head=head, send=send, c=combine, x=x_phase, d=d_phase,
            y=y_phase, g=gather, w=w_phase, s1=sum_1, s2=sum_2, s3=sum_3,
        )

        def run(name, *args):
            with jax.named_scope(name + "_" + "_".join(map(str, args))):
                ph[name](*args)

        def proj(l, g, c):
            with jax.named_scope(f"proj_{l}_{g}_{c}"):
                project(l, (g,), c)
            send(l, g, c)

        groups, A, B = range(n_g), 0, 1
        for g in groups:
            start(*[("r", g, b) for b in range(n_tx)])
        start("nw")
        for k in range(1, n_tx):
            pl.semaphore_signal(barrier, 1, device_id=tx_of(lax.rem(me + k, n_tx)), device_id_type=MESH)
            pl.semaphore_signal(barrier, 1, device_id=(dp, lax.rem(me + k, n_tx), partner_ty), device_id_type=MESH)
        for k in range(1, n_ty):
            pl.semaphore_signal(barrier, 1, device_id=ty_of(lax.rem(ty + k, n_ty)), device_id_type=MESH)
        for g in groups:
            wait(*[("r", g, b) for b in range(n_tx)])
        wait("nw")
        start(*[("win", 0, t) for t in range(n_w)])
        pl.semaphore_wait(barrier, 2 * (n_tx - 1) + n_ty - 1)
        for g in groups:
            run("stat", 0, g)
        start("cw", "cb", "db", "al", "ds", "cs", ("wx", 0), ("wdt", 0), ("ss", 0), ("wout", 0))
        def each(name, l, g, *cs):
            for c in cs:
                run(name, l, g, c)

        for l in range(n_layer):
            p = l - 1
            run("head", l, A)
            proj(l, A, 0)
            if l == 0:
                proj(l, A, 1)
                proj(l, A, 2)
                each("c", l, A, 0)
                proj(l, A, 3)
                each("send", l, A, 4, 5, 6, 7)
                run("head", l, B)
                proj(l, B, 0)
                each("c", l, A, 1, 2)
                proj(l, B, 1)
                each("c", l, A, 3)
                proj(l, B, 2)
                start(*[("win", 1, t) for t in range(n_w)])
                start(("wx", 1), ("wdt", 1), ("ss", 1), ("wout", 1))
                wait("cw", "cb", "db", "al", "ds", "cs", ("wx", 0))
                al[...] = -jnp.exp(al[...]) * LOG2E
                each("c", l, A, 4)
                proj(l, B, 3)
                each("send", l, B, 4, 5)
                each("c", l, A, 5)
                run("x", l, A)
                each("c", l, A, 6, 7)
                each("c", l, B, 0, 1)
            else:
                proj(l, A, 1)
                each("g", p, B, 0, 1, 2, 3)
                proj(l, A, 2)
                each("w", p, B, 0, 1, 2, 3)
                proj(l, A, 3)
                each("c", l, A, 0)
                run("s1", p, B)
                each("c", l, A, 1, 2)
                run("s2", p, B)
                run("stat", l, B)
                each("send", l, A, 4, 5, 6, 7)
                each("c", l, A, 3)
                run("s3", p, B)
                wait(("wx", l))
                run("x", l, A)
                run("head", l, B)
                proj(l, B, 0)
                each("c", l, A, 4)
                proj(l, B, 1)
                each("c", l, A, 5, 6)
                proj(l, B, 2)
                each("c", l, A, 7)
                each("c", l, B, 0)
                proj(l, B, 3)
                each("send", l, B, 4, 5)
                each("c", l, B, 1)
            wait(("wdt", l), ("ss", l))
            run("d", l, A)
            each("c", l, B, 2, 3)
            each("y", l, A, 0, 1, 2, 3)
            each("send", l, B, 6, 7)
            if l == 0:
                each("c", l, B, 4)
                each("g", l, A, 0, 1, 2, 3)
                run("x", l, B)
            else:
                run("x", l, B)
                each("c", l, B, 4)
                each("g", l, A, 0, 1, 2, 3)
            each("c", l, B, 5, 6, 7)
            wait(("wout", l))
            if l == 0:
                each("w", l, A, 0, 1, 2, 3)
                run("s1", l, A)
                run("d", l, B)
                run("s2", l, A)
                run("stat", l + 1, A)
                each("y", l, B, 0, 1, 2, 3)
                run("s3", l, A)
            else:
                run("d", l, B)
                each("y", l, B, 0, 1, 2, 3)
                each("w", l, A, 0, 1, 2, 3)
                run("s1", l, A)
        p = n_layer - 1
        each("g", p, B, 0, 1)
        each("w", p, B, 0)
        each("g", p, B, 2)
        each("w", p, B, 1)
        each("g", p, B, 3)
        run("s2", p, A)
        each("w", p, B, 2, 3)
        run("s3", p, A)
        run("s1", p, B)
        run("s2", p, B)
        run("s3", p, B)

        with jax.named_scope("end"):
            all_of(own.at[:, :, :, pl.ds(0, 3)], rs_s, fn_r.at[0, 0, 0]).wait_send()
            all_of(sti, st_s, fn_r.at[0, 0, 0]).wait_send()
            all_of(pin, p_s, fn_r.at[0, 0, 0]).wait_send()
            all_of(so, s_s, fn_r.at[0, 0, 0]).wait_send()

            @pl.when(mid == 0)
            def _():
                all_of(yall.at[:, :, :, pl.ds(0, 2)], ag_s, fn_r.at[0, 0, 0]).wait_send()

            @pl.when(mid == 1)
            def _():
                all_of(yall, ag_s, fn_r.at[0, 0, 0]).wait_send()

    def dma(*s):
        return pltpu.SemaphoreType.DMA(s) if s else pltpu.SemaphoreType.DMA

    def vm(t, *s):
        return pltpu.VMEM(s, t)

    nl, p_w = n_layer, rank + 2 * n_state
    scratch = [
        vm(F32, nl, d_loc), vm(BF16, nl, n_w, d_loc, 2, 128), vm(F32, nl, 4, chan), vm(F32, nl, chan),
        vm(BF16, nl, p_w, chan), vm(BF16, nl, rank, chan), vm(F32, nl, chan), vm(F32, nl, n_state, chan), vm(F32, nl, chan),
        vm(BF16, nl, chan, d_loc),
        vm(BF16, n_g, 2 * rg, 2 * d_loc), vm(BF16, nl, n_g, 2 * n_c, n_tx, hb, chunk),
        vm(BF16, nl, n_g, 2 * n_c, 2, hb, chunk), vm(BF16, nl, n_g, 2 * n_c, 2, hb, chunk),
        vm(F32, n_g, hb, chan), vm(F32, hb, chan), vm(F32, hb, chan), vm(F32, n_g, hb, chan),
        vm(F32, 2, hb, n_state, 128), vm(BF16, nl, n_g, hb, p_w), vm(BF16, nl, n_g, n_ty - 1, hb, p_w),
        vm(BF16, nl, n_g, n_c, n_tx, hb, chunk), vm(F32, n_g, rg, d_loc),
        vm(BF16, 3, nl, n_g, n_q, half, qw), vm(BF16, 3, nl, n_g, n_q, half, qw),
        vm(F32, nl, n_g, 8, half), vm(F32, nl, n_g, 2 * n_tx - 1, 8, half), vm(F32, rg, 128),
        dma(7 + 4 * nl), dma(n_g, n_tx), dma(nl, n_w),
        dma(), dma(nl, n_g, 2 * n_c), dma(nl, n_g, 2 * n_c),
        dma(), dma(nl, n_g), dma(), dma(nl, n_g, n_c, 2),
        dma(), dma(nl, n_g, 3, n_q), dma(), dma(nl, n_g),
    ]
    outs = (vm(F32, n_g, rg, d_loc), vm(BF16, nl, blk, chan), vm(BF16, nl, 3, blk, chan), vm(F32, nl, blk, n_state, chan))
    return kernel, outs, scratch


def store_kernel(r, xi, cs, ss, r_out, conv_out, ssm_out, sem):
    n_g, rg, _ = r.shape
    nl, blk = ss.shape[:2]
    hb = blk // n_g
    pairs = []
    for l in range(nl):
        for i in range(0, blk, 8):
            pairs.append((ss.at[l, pl.ds(i, 8)], ssm_out.at[l, pl.ds(i, 8)]))
    for l in range(nl):
        pairs.append((cs.at[l, pl.ds(1, 2)], conv_out.at[l, pl.ds(0, 2)]))
        pairs.append((xi.at[l], conv_out.at[l, 2]))
    for g in range(n_g):
        for b in range(rg // hb):
            pairs.append((r.at[g, pl.ds(b * hb, hb)], r_out.at[pl.ds(b * blk + g * hb, hb)]))
    copies = [pltpu.make_async_copy(src, dst, sem.at[i]) for i, (src, dst) in enumerate(pairs)]
    for cp in copies:
        cp.start()
    for cp in copies:
        cp.wait()


def solution(mesh):
    n_tx, n_ty = mesh.shape["tx"], mesh.shape["ty"]

    def local_step(residual, norm_w, w_in, conv_w, conv_b, w_x, w_dt, dt_bias, a_log, d_skip, w_out, conv_state, ssm_state):
        rows, d_loc = residual.shape
        n_layer, _, _, chan = w_in.shape
        rank, n_state = w_dt.shape[1], a_log.shape[-1]
        blk = rows // n_tx
        kernel, outs, scratch = make_kernel(n_layer, n_tx, n_ty, rows, d_loc, chan, rank, n_state, 512, 2, 2)
        parts = pl.pallas_call(
            kernel,
            out_shape=outs,
            in_specs=[ANY] * 13,
            out_specs=(VMEM,) * 4,
            scratch_shapes=scratch,
            compiler_params=pltpu.CompilerParams(collective_id=0, has_side_effects=True, vmem_limit_bytes=67043328 - 11 * 2**20),
            name="mixer",
        )(
            residual, norm_w, w_in, conv_w.transpose(0, 2, 1), conv_b, w_x.transpose(0, 2, 1), w_dt, dt_bias,
            a_log.transpose(0, 2, 1), d_skip, w_out, conv_state.transpose(0, 3, 1, 2), ssm_state.transpose(0, 1, 3, 2),
        )
        r_out, conv_out, ssm_out = pl.pallas_call(
            store_kernel,
            out_shape=(
                jax.ShapeDtypeStruct((rows, d_loc), F32),
                jax.ShapeDtypeStruct((n_layer, 3, blk, chan), BF16),
                jax.ShapeDtypeStruct((n_layer, blk, n_state, chan), F32),
            ),
            in_specs=[VMEM] * 4,
            out_specs=(ANY,) * 3,
            scratch_shapes=[pltpu.SemaphoreType.DMA((64,))],
            compiler_params=pltpu.CompilerParams(vmem_limit_bytes=12 * 2**20),
            name="store",
        )(*parts)
        return r_out, conv_out.transpose(0, 2, 3, 1), ssm_out.transpose(0, 1, 3, 2)

    cache_spec = P(None, ("dp", "tx"), "ty", None)
    in_specs = (P("dp", "tx"), P(None, "tx"), P(None, "tx", None, "ty"), P(None, "ty", None), P(None, "ty"), P(None, "ty", None), P(None, None, "ty"), P(None, "ty"), P(None, "ty", None), P(None, "ty"), P(None, "ty", "tx"), cache_spec, cache_spec)
    out_specs = (P("dp", "tx"), cache_spec, cache_spec)
    return jax.shard_map(local_step, mesh=mesh, in_specs=in_specs, out_specs=out_specs, check_vma=False)
```

time: 111 us -> 96 us (0.86)
  Pallas kernels: 111 us -> 95 us
    pallas_call x1, Pallas kernels: 106 us -> 90.8 us  [local_step(): pl.pallas_call(kernel, out_shape=outs, in_specs=[ANY] * 13, out_specs=(VM...]
where the time goes in v3:
time: 96 us; the launch traced here: 95.8 us
  Pallas kernels  95 us (99%)
    pallas_call x1, Pallas kernels, local_step(): pl.pallas_call(kernel, out_shape=outs, in_specs=[ANY] * 13, out_specs=(VM...  90.8 us
    pallas_call x1, Pallas kernels, local_step(): pl.pallas_call(store_kernel, out_shape=(jax.ShapeDtypeStruct((rows, d_loc...  4.22 us

profile of v3, /device:TPU:0, one launch (start us, length us, event | category | flops | bytes accessed | tf_op | source)
XLA Modules:
  0.0 95.8 jit_solution(17415860417388687813)
XLA Ops:
  0.6 90.8 %mixer.1 = (f32[2,64,1024]{2,1,0:T(8,128)S(1)}, bf16[2,32,2048]{2,1,0:T(8,128)(2,1)S(1)}, bf16[2,3,32,2048]{3,2,1,0:T(8,128)(2,1)S(1)}, f32[2,32,16,2048]{3,2,1,0:T(8,128)S(1)}) custom-call(f32[128,1024]{1,0:T(8,128)} %r_hbm.1, f32[2,1024]{1,0:T(2,128)} %nw_hbm.1, bf16[2,1024,2,2048]{3,2,1,0:T(2,128)(2,1)} %win_hbm.1, f32[2,4,2048]{2,1,0:T(4,128)} %bitcast.11, ...), custom_call_target="tpu_custom_call" | custom-call | tf_op jit(solution)/shard_map/mixer/pallas_call | solution.py:475
  91.4 4.2 %store.1 = (f32[128,1024]{1,0:T(8,128)}, bf16[2,3,32,2048]{3,2,1,0:T(8,128)(2,1)}, f32[2,32,16,2048]{3,2,1,0:T(8,128)}) custom-call(f32[2,64,1024]{2,1,0:T(8,128)S(1)} %get-tuple-element.10.r, bf16[2,32,2048]{2,1,0:T(8,128)(2,1)S(1)} %get-tuple-element.11.xi, bf16[2,3,32,2048]{3,2,1,0:T(8,128)(2,1)S(1)} %get-tuple-element.12.cs, ...), custom_call_target="tpu_custom_call" | custom-call | tf_op jit(solution)/shard_map/store/pallas_call | solution.py:487

commit v4 on v3

--- a/solution.py
+++ b/solution.py
@@ -32,7 +32,7 @@
         r_hbm, nw_hbm, win_hbm, cw_hbm, cb_hbm, wx_hbm, wdt_hbm, db_hbm, al_hbm, ds_hbm, wout_hbm, cs_hbm, ss_hbm,
         r, xi, cs, ss,
         nw, win, cw, cb, wx, wdt, db, al, ds, wout,
-        hx, own, cmb, fin, xc, dt, dx, sv, bc, pown, pin, yall, acc, so, si, sto, sti, sc,
+        hx, own, cmb, fin, xc, dt, dx, sv, bc, dl, pown, pin, yall, acc, so, si, sto, sti, sc, sl, pf,
         ld_sem, r_sem, win_sem, rs_s, cm_r, fn_r, p_s, p_r, ag_s, ag_r, s_s, s_r, st_s, st_r,
     ):
         dp, me, ty = lax.axis_index("dp"), lax.axis_index("tx"), lax.axis_index("ty")
@@ -116,13 +116,12 @@
                         stat_copy(l, g, j, rel).start()
 
         def head(l, g):
-            all_of(sti.at[l, g], st_s, st_r.at[l, g]).wait_recv()
-            for rel, at in enumerate((mine, other)):
-                tot = sto[l, g] if rel == 0 else sti[l, g, 0]
-                for j in range(1, n_tx):
-                    tot = tot + sti[l, g, 2 * j + rel - 1]
-                sc[at, :] = lax.rsqrt(jnp.broadcast_to(tot[0:1, :], (128, half)).T / d_model + NORM_EPS)
-            scale = sc[...]
+            for b in range(2):
+                at = pl.ds(b * half, half)
+                part = r[g, at, :]
+                sq = jnp.sum(part * part, axis=-1, keepdims=True)
+                sl[g, at, :] = lax.rsqrt(jnp.broadcast_to(sq, (half, 128)) / d_model + NORM_EPS)
+            scale = sl[g]
             row_i = lax.broadcasted_iota(jnp.int32, (128, 256), 0)
             col_i = lax.broadcasted_iota(jnp.int32, (128, 256), 1)
             pick = [(col_i == 2 * row_i + k).astype(F32).astype(BF16) for k in range(2)]
@@ -132,19 +131,36 @@
                 for k in range(2):
                     hx[g, k * rg : (k + 1) * rg, pl.ds(j * 256, 256)] = dot(h, pick[k]).astype(BF16)
 
-        def project(l, gs, c):
-            lhs = hx[gs[0]] if len(gs) == 1 else hx[...].reshape(n_g * 2 * rg, 2 * d_loc)
+        def norm(l, g):
+            all_of(sti.at[l, g], st_s, st_r.at[l, g]).wait_recv()
+            for rel, at in enumerate((mine, other)):
+                tot = sto[l, g] if rel == 0 else sti[l, g, 0]
+                for j in range(1, n_tx):
+                    tot = tot + sti[l, g, 2 * j + rel - 1]
+                sc[at, :] = lax.rsqrt(jnp.broadcast_to(tot[0:1, :], (128, half)).T / d_model + NORM_EPS)
+            sl[g] = jnp.where(sl[g] > 0.0, sc[...] / sl[g], 0.0)
+
+        def project(l, g, c, early):
             for t in range(0, chunk // 128, 2):
                 tile = c * (chunk // 128) + t
-                if gs[0] == 0:
-                    wait(("win", l, tile), ("win", l, tile + 1))
                 w = jnp.concatenate([win.at[l, tile + i].reshape(2 * d_loc, 128)[...] for i in range(2)], axis=1)
-                part = dot(lhs, w).astype(BF16)
-                for i, g in enumerate(gs):
-                    for k in range(2):
-                        for b in range(n_tx):
-                            at = (2 * i + k) * rg + b * hb
-                            own[l, g, k * n_c + c, b, :, pl.ds(t * 128, 256)] = part[at : at + hb, :]
+                part = dot(hx[g], w)
+                if early:
+                    pf[c, :, pl.ds(t * 128, 256)] = part
+                else:
+                    scaled(l, g, c, t, part)
+
+        def scaled(l, g, c, t, part):
+            ratio = jnp.concatenate([sl[g], sl[g]], axis=1)
+            for k in range(2):
+                piece = (part[k * rg : (k + 1) * rg, :] * ratio).astype(BF16)
+                for b in range(n_tx):
+                    own[l, g, k * n_c + c, b, :, pl.ds(t * 128, 256)] = piece[b * hb : (b + 1) * hb, :]
+
+        def out(l, g, c):
+            for t in range(0, chunk // 128, 2):
+                scaled(l, g, c, t, pf[c, :, pl.ds(t * 128, 256)])
+            send(l, g, c)
 
         def send(l, g, c):
             @pl.when(mid == 0)
@@ -193,26 +209,29 @@
                 mat = p_sum[:, rank + i * n_state : rank + (i + 1) * n_state]
                 mat_t = (mat * lax.rsqrt(jnp.mean(mat * mat, axis=-1, keepdims=True) + INNER_EPS)).T
                 for b in range(hb):
-                    bc[i, b] = jnp.broadcast_to(mat_t[:, b : b + 1], (n_state, 128))
-            for c in range(n_c):
-                cols = pl.ds(c * chunk, chunk)
-                raw = dot(dt_low, wdt[l, :, cols]) + db[l : l + 1, cols]
-                delta = jnp.maximum(raw, 0.0) + jnp.log1p(jnp.exp(-jnp.abs(raw)))
-                dt[:, cols] = delta
-                dx[:, cols] = delta * xc[g, :, cols]
-                neg_a = al[l, :, cols]
-
-                def row_step(b, carry):
-                    row = pl.ds(b, 1)
-                    b_row = jnp.concatenate([bc[0, b]] * (chunk // 128), axis=1)
-                    c_row = jnp.concatenate([bc[1, b]] * (chunk // 128), axis=1)
-                    at = g * hb + b
-                    s_new = jnp.exp2(dt[row, cols] * neg_a) * ss[l, at, :, cols] + dx[row, cols] * b_row
-                    ss[l, at, :, cols] = s_new
-                    sv[g, row, cols] = jnp.sum(s_new * c_row, axis=0, keepdims=True)
-                    return carry
-
-                lax.fori_loop(0, hb, row_step, 0, unroll=4)
+                    bc[g, i, b] = jnp.broadcast_to(mat_t[:, b : b + 1], (n_state, 128))
+            dl[g] = dt_low
+
+        def d_chunk(l, g, c):
+            cols = pl.ds(c * chunk, chunk)
+            dt_low = dl[g]
+            raw = dot(dt_low, wdt[l, :, cols]) + db[l : l + 1, cols]
+            delta = jnp.maximum(raw, 0.0) + jnp.log1p(jnp.exp(-jnp.abs(raw)))
+            dt[:, cols] = delta
+            dx[:, cols] = delta * xc[g, :, cols]
+            neg_a = al[l, :, cols]
+
+            def row_step(b, carry):
+                row = pl.ds(b, 1)
+                b_row = jnp.concatenate([bc[g, 0, b]] * (chunk // 128), axis=1)
+                c_row = jnp.concatenate([bc[g, 1, b]] * (chunk // 128), axis=1)
+                at = g * hb + b
+                s_new = jnp.exp2(dt[row, cols] * neg_a) * ss[l, at, :, cols] + dx[row, cols] * b_row
+                ss[l, at, :, cols] = s_new
+                sv[g, row, cols] = jnp.sum(s_new * c_row, axis=0, keepdims=True)
+                return carry
+
+            lax.fori_loop(0, hb, row_step, 0, unroll=4)
 
         def y_phase(l, g, c):
             cols = pl.ds(c * chunk, chunk)
@@ -224,12 +243,14 @@
             def _():
                 ag_copy(l, g, c, me, 0, o_mid).start()
 
-            ag_copy(l, g, c, me, 1, mate).start()
-
             @pl.when(mid == 1)
             def _():
                 ag_copy(l, g, c, me, 1, o_end).start()
                 ag_copy(l, g, c, me, 1, o_mid).start()
+
+        def y_mate(l, g):
+            for c in range(n_c):
+                ag_copy(l, g, c, me, 1, mate).start()
 
         def gather(l, g, c):
             @pl.when(mid == 1)
@@ -272,18 +293,19 @@
                 r[g, other, pl.ds(q * qw, qw)] += si[2, l, g, q].astype(F32)
 
         ph = dict(
-            stat=stat, head=head, send=send, c=combine, x=x_phase, d=d_phase,
-            y=y_phase, g=gather, w=w_phase, s1=sum_1, s2=sum_2, s3=sum_3,
+            stat=stat, head=head, norm=norm, out=out, send=send, c=combine, x=x_phase, d=d_phase, dc=d_chunk,
+            y=y_phase, ym=y_mate, g=gather, w=w_phase, s1=sum_1, s2=sum_2, s3=sum_3,
         )
 
         def run(name, *args):
             with jax.named_scope(name + "_" + "_".join(map(str, args))):
                 ph[name](*args)
 
-        def proj(l, g, c):
+        def proj(l, g, c, early=False):
             with jax.named_scope(f"proj_{l}_{g}_{c}"):
-                project(l, (g,), c)
-            send(l, g, c)
+                project(l, g, c, early)
+            if not early:
+                send(l, g, c)
 
         groups, A, B = range(n_g), 0, 1
         for g in groups:
@@ -306,100 +328,123 @@
             for c in cs:
                 run(name, l, g, c)
 
-        for l in range(n_layer):
-            p = l - 1
-            run("head", l, A)
-            proj(l, A, 0)
-            if l == 0:
-                proj(l, A, 1)
-                proj(l, A, 2)
-                each("c", l, A, 0)
-                proj(l, A, 3)
-                each("send", l, A, 4, 5, 6, 7)
-                run("head", l, B)
-                proj(l, B, 0)
-                each("c", l, A, 1, 2)
-                proj(l, B, 1)
-                each("c", l, A, 3)
-                proj(l, B, 2)
-                start(*[("win", 1, t) for t in range(n_w)])
-                start(("wx", 1), ("wdt", 1), ("ss", 1), ("wout", 1))
-                wait("cw", "cb", "db", "al", "ds", "cs", ("wx", 0))
-                al[...] = -jnp.exp(al[...]) * LOG2E
-                each("c", l, A, 4)
-                proj(l, B, 3)
-                each("send", l, B, 4, 5)
-                each("c", l, A, 5)
-                run("x", l, A)
-                each("c", l, A, 6, 7)
-                each("c", l, B, 0, 1)
-            else:
-                proj(l, A, 1)
-                each("g", p, B, 0, 1, 2, 3)
-                proj(l, A, 2)
-                each("w", p, B, 0, 1, 2, 3)
-                proj(l, A, 3)
-                each("c", l, A, 0)
-                run("s1", p, B)
-                each("c", l, A, 1, 2)
-                run("s2", p, B)
-                run("stat", l, B)
-                each("send", l, A, 4, 5, 6, 7)
-                each("c", l, A, 3)
-                run("s3", p, B)
-                wait(("wx", l))
-                run("x", l, A)
-                run("head", l, B)
-                proj(l, B, 0)
-                each("c", l, A, 4)
-                proj(l, B, 1)
-                each("c", l, A, 5, 6)
-                proj(l, B, 2)
-                each("c", l, A, 7)
-                each("c", l, B, 0)
-                proj(l, B, 3)
-                each("send", l, B, 4, 5)
-                each("c", l, B, 1)
-            wait(("wdt", l), ("ss", l))
-            run("d", l, A)
-            each("c", l, B, 2, 3)
-            each("y", l, A, 0, 1, 2, 3)
-            each("send", l, B, 6, 7)
-            if l == 0:
-                each("c", l, B, 4)
-                each("g", l, A, 0, 1, 2, 3)
-                run("x", l, B)
-            else:
-                run("x", l, B)
-                each("c", l, B, 4)
-                each("g", l, A, 0, 1, 2, 3)
-            each("c", l, B, 5, 6, 7)
-            wait(("wout", l))
-            if l == 0:
-                each("w", l, A, 0, 1, 2, 3)
-                run("s1", l, A)
-                run("d", l, B)
-                run("s2", l, A)
-                run("stat", l + 1, A)
-                each("y", l, B, 0, 1, 2, 3)
-                run("s3", l, A)
-            else:
-                run("d", l, B)
-                each("y", l, B, 0, 1, 2, 3)
-                each("w", l, A, 0, 1, 2, 3)
-                run("s1", l, A)
-        p = n_layer - 1
-        each("g", p, B, 0, 1)
-        each("w", p, B, 0)
-        each("g", p, B, 2)
-        each("w", p, B, 1)
-        each("g", p, B, 3)
-        run("s2", p, A)
-        each("w", p, B, 2, 3)
-        run("s3", p, A)
-        run("s1", p, B)
-        run("s2", p, B)
-        run("s3", p, B)
+        def d_all(l, g):
+            run("d", l, g)
+            each("dc", l, g, 0, 1, 2, 3)
+
+        run("head", 0, A)
+        wait(*[("win", 0, t) for t in range(n_w // 2)])
+        proj(0, A, 0, True)
+        proj(0, A, 1, True)
+        run("norm", 0, A)
+        each("out", 0, A, 0, 1)
+        wait(*[("win", 0, t) for t in range(n_w // 2, n_w)])
+        proj(0, A, 2)
+        proj(0, A, 3)
+        each("send", 0, A, 4, 5, 6, 7)
+        run("head", 0, B)
+        run("norm", 0, B)
+        each("c", 0, A, 0)
+        proj(0, B, 0)
+        each("c", 0, A, 1)
+        proj(0, B, 1)
+        each("c", 0, A, 2)
+        proj(0, B, 2)
+        start(*[("win", 1, t) for t in range(n_w)])
+        start(("wx", 1), ("wdt", 1), ("ss", 1), ("wout", 1))
+        wait("cw", "cb", "db", "al", "ds", "cs", ("wx", 0))
+        al[...] = -jnp.exp(al[...]) * LOG2E
+        each("c", 0, A, 3)
+        proj(0, B, 3)
+        each("send", 0, B, 4)
+        each("c", 0, A, 4, 5)
+        run("x", 0, A)
+        each("c", 0, A, 6, 7)
+        each("c", 0, B, 0, 1)
+        wait(("wdt", 0), ("ss", 0))
+        run("d", 0, A)
+        each("dc", 0, A, 0, 1)
+        each("c", 0, B, 2)
+        each("dc", 0, A, 2, 3)
+        each("c", 0, B, 3)
+        each("y", 0, A, 0, 1, 2, 3)
+        run("ym", 0, A)
+        each("send", 0, B, 5, 6, 7)
+        each("c", 0, B, 4)
+        each("g", 0, A, 0, 1)
+        run("x", 0, B)
+        each("g", 0, A, 2, 3)
+        each("c", 0, B, 5, 6, 7)
+        wait(("wout", 0))
+        each("w", 0, A, 0, 1, 2, 3)
+        run("s1", 0, A)
+        d_all(0, B)
+        run("s2", 0, A)
+        run("stat", 1, A)
+        each("y", 0, B, 0, 1, 2, 3)
+        run("ym", 0, B)
+        run("s3", 0, A)
+        wait(*[("win", 1, t) for t in range(n_w)])
+        run("head", 1, A)
+        proj(1, A, 0, True)
+        proj(1, A, 1, True)
+        run("norm", 1, A)
+        each("out", 1, A, 0, 1)
+        each("g", 0, B, 0, 1)
+        proj(1, A, 2)
+        each("g", 0, B, 2, 3)
+        proj(1, A, 3)
+        each("w", 0, B, 0, 1, 2, 3)
+        each("c", 1, A, 0, 1)
+        run("s1", 0, B)
+        each("c", 1, A, 2, 3)
+        run("s2", 0, B)
+        run("stat", 1, B)
+        each("send", 1, A, 4, 5, 6, 7)
+        run("s3", 0, B)
+        run("head", 1, B)
+        proj(1, B, 0, True)
+        proj(1, B, 1, True)
+        wait(("wx", 1))
+        run("x", 1, A)
+        run("norm", 1, B)
+        each("out", 1, B, 0, 1)
+        proj(1, B, 2)
+        each("c", 1, A, 4, 5)
+        proj(1, B, 3)
+        each("send", 1, B, 4, 5, 6, 7)
+        each("c", 1, A, 6, 7)
+        wait(("wdt", 1), ("ss", 1))
+        run("d", 1, A)
+        each("dc", 1, A, 0, 1)
+        each("c", 1, B, 0)
+        each("dc", 1, A, 2, 3)
+        each("c", 1, B, 1, 2, 3)
+        each("y", 1, A, 0, 1, 2, 3)
+        run("ym", 1, A)
+        each("c", 1, B, 4, 5)
+        run("x", 1, B)
+        each("c", 1, B, 6, 7)
+        each("g", 1, A, 0, 1, 2, 3)
+        run("d", 1, B)
+        for c in range(n_c):
+            run("dc", 1, B, c)
+            run("y", 1, B, c)
+        run("ym", 1, B)
+        wait(("wout", 1))
+        each("w", 1, A, 0, 1, 2, 3)
+        each("g", 1, B, 0, 1)
+        run("s1", 1, A)
+        each("w", 1, B, 0)
+        each("g", 1, B, 2)
+        each("w", 1, B, 1)
+        each("g", 1, B, 3)
+        each("w", 1, B, 2, 3)
+        run("s2", 1, A)
+        run("s1", 1, B)
+        run("s3", 1, A)
+        run("s2", 1, B)
+        run("s3", 1, B)
 
         with jax.named_scope("end"):
             all_of(own.at[:, :, :, pl.ds(0, 3)], rs_s, fn_r.at[0, 0, 0]).wait_send()
@@ -429,10 +474,10 @@
         vm(BF16, n_g, 2 * rg, 2 * d_loc), vm(BF16, nl, n_g, 2 * n_c, n_tx, hb, chunk),
         vm(BF16, nl, n_g, 2 * n_c, 2, hb, chunk), vm(BF16, nl, n_g, 2 * n_c, 2, hb, chunk),
         vm(F32, n_g, hb, chan), vm(F32, hb, chan), vm(F32, hb, chan), vm(F32, n_g, hb, chan),
-        vm(F32, 2, hb, n_state, 128), vm(BF16, nl, n_g, hb, p_w), vm(BF16, nl, n_g, n_ty - 1, hb, p_w),
+        vm(F32, n_g, 2, hb, n_state, 128), vm(BF16, n_g, hb, rank), vm(BF16, nl, n_g, hb, p_w), vm(BF16, nl, n_g, n_ty - 1, hb, p_w),
         vm(BF16, nl, n_g, n_c, n_tx, hb, chunk), vm(F32, n_g, rg, d_loc),
         vm(BF16, 3, nl, n_g, n_q, half, qw), vm(BF16, 3, nl, n_g, n_q, half, qw),
-        vm(F32, nl, n_g, 8, half), vm(F32, nl, n_g, 2 * n_tx - 1, 8, half), vm(F32, rg, 128),
+        vm(F32, nl, n_g, 8, half), vm(F32, nl, n_g, 2 * n_tx - 1, 8, half), vm(F32, rg, 128), vm(F32, n_g, rg, 128), vm(F32, 2, 2 * rg, chunk),
         dma(7 + 4 * nl), dma(n_g, n_tx), dma(nl, n_w),
         dma(), dma(nl, n_g, 2 * n_c), dma(nl, n_g, 2 * n_c),
         dma(), dma(nl, n_g), dma(), dma(nl, n_g, n_c, 2),

time: 96 us -> 90.7 us (0.945)
  Pallas kernels: 95 us -> 89.5 us
    pallas_call x1, Pallas kernels: 90.8 us -> 85.3 us  [local_step(): pl.pallas_call(kernel, out_shape=outs, in_specs=[ANY] * 13, out_specs=(VM...]
where the time goes in v4:
time: 90.7 us; the launch traced here: 90.3 us
  Pallas kernels  89.5 us (99%)
    pallas_call x1, Pallas kernels, local_step(): pl.pallas_call(kernel, out_shape=outs, in_specs=[ANY] * 13, out_specs=(VM...  85.3 us
    pallas_call x1, Pallas kernels, local_step(): pl.pallas_call(store_kernel, out_shape=(jax.ShapeDtypeStruct((rows, d_loc...  4.22 us

profile of v4, /device:TPU:0, one launch (start us, length us, event | category | flops | bytes accessed | tf_op | source)
XLA Modules:
  0.0 90.3 jit_solution(147323599982626098)
XLA Ops:
  0.6 85.3 %mixer.1 = (f32[2,64,1024]{2,1,0:T(8,128)S(1)}, bf16[2,32,2048]{2,1,0:T(8,128)(2,1)S(1)}, bf16[2,3,32,2048]{3,2,1,0:T(8,128)(2,1)S(1)}, f32[2,32,16,2048]{3,2,1,0:T(8,128)S(1)}) custom-call(f32[128,1024]{1,0:T(8,128)} %r_hbm.1, f32[2,1024]{1,0:T(2,128)} %nw_hbm.1, bf16[2,1024,2,2048]{3,2,1,0:T(2,128)(2,1)} %win_hbm.1, f32[2,4,2048]{2,1,0:T(4,128)} %bitcast.11, ...), custom_call_target="tpu_custom_call" | custom-call | tf_op jit(solution)/shard_map/mixer/pallas_call | solution.py:520
  85.9 4.2 %store.1 = (f32[128,1024]{1,0:T(8,128)}, bf16[2,3,32,2048]{3,2,1,0:T(8,128)(2,1)}, f32[2,32,16,2048]{3,2,1,0:T(8,128)}) custom-call(f32[2,64,1024]{2,1,0:T(8,128)S(1)} %get-tuple-element.10.r, bf16[2,32,2048]{2,1,0:T(8,128)(2,1)S(1)} %get-tuple-element.11.xi, bf16[2,3,32,2048]{3,2,1,0:T(8,128)(2,1)S(1)} %get-tuple-element.12.cs, ...), custom_call_target="tpu_custom_call" | custom-call | tf_op jit(solution)/shard_map/store/pallas_call | solution.py:532

commit v5 on v4

--- a/solution.py
+++ b/solution.py
@@ -328,123 +328,121 @@
             for c in cs:
                 run(name, l, g, c)
 
-        def d_all(l, g):
-            run("d", l, g)
-            each("dc", l, g, 0, 1, 2, 3)
-
-        run("head", 0, A)
-        wait(*[("win", 0, t) for t in range(n_w // 2)])
-        proj(0, A, 0, True)
-        proj(0, A, 1, True)
-        run("norm", 0, A)
-        each("out", 0, A, 0, 1)
-        wait(*[("win", 0, t) for t in range(n_w // 2, n_w)])
-        proj(0, A, 2)
-        proj(0, A, 3)
-        each("send", 0, A, 4, 5, 6, 7)
-        run("head", 0, B)
-        run("norm", 0, B)
-        each("c", 0, A, 0)
-        proj(0, B, 0)
-        each("c", 0, A, 1)
-        proj(0, B, 1)
-        each("c", 0, A, 2)
-        proj(0, B, 2)
-        start(*[("win", 1, t) for t in range(n_w)])
-        start(("wx", 1), ("wdt", 1), ("ss", 1), ("wout", 1))
-        wait("cw", "cb", "db", "al", "ds", "cs", ("wx", 0))
+        X, Z = range(n_c), range(n_c, 2 * n_c)
+        head2, tail2, l0, l1 = X[:2], X[2:], 0, n_layer - 1
+        early = n_w // 2
+
+        run("head", l0, A)
+        wait(*[("win", l0, t) for t in range(early)])
+        for c in head2:
+            proj(l0, A, c, True)
+        run("norm", l0, A)
+        each("out", l0, A, *head2)
+        wait(*[("win", l0, t) for t in range(early, n_w)])
+        for c in tail2:
+            proj(l0, A, c)
+        each("send", l0, A, *Z)
+        run("head", l0, B)
+        run("norm", l0, B)
+        for c in X[:-1]:
+            run("c", l0, A, c)
+            proj(l0, B, c)
+        start(*[("win", l1, t) for t in range(n_w)])
+        start(("wx", l1), ("wdt", l1), ("ss", l1), ("wout", l1))
+        wait("cw", "cb", "db", "al", "ds", "cs", ("wx", l0))
         al[...] = -jnp.exp(al[...]) * LOG2E
-        each("c", 0, A, 3)
-        proj(0, B, 3)
-        each("send", 0, B, 4)
-        each("c", 0, A, 4, 5)
-        run("x", 0, A)
-        each("c", 0, A, 6, 7)
-        each("c", 0, B, 0, 1)
-        wait(("wdt", 0), ("ss", 0))
-        run("d", 0, A)
-        each("dc", 0, A, 0, 1)
-        each("c", 0, B, 2)
-        each("dc", 0, A, 2, 3)
-        each("c", 0, B, 3)
-        each("y", 0, A, 0, 1, 2, 3)
-        run("ym", 0, A)
-        each("send", 0, B, 5, 6, 7)
-        each("c", 0, B, 4)
-        each("g", 0, A, 0, 1)
-        run("x", 0, B)
-        each("g", 0, A, 2, 3)
-        each("c", 0, B, 5, 6, 7)
-        wait(("wout", 0))
-        each("w", 0, A, 0, 1, 2, 3)
-        run("s1", 0, A)
-        d_all(0, B)
-        run("s2", 0, A)
-        run("stat", 1, A)
-        each("y", 0, B, 0, 1, 2, 3)
-        run("ym", 0, B)
-        run("s3", 0, A)
-        wait(*[("win", 1, t) for t in range(n_w)])
-        run("head", 1, A)
-        proj(1, A, 0, True)
-        proj(1, A, 1, True)
-        run("norm", 1, A)
-        each("out", 1, A, 0, 1)
-        each("g", 0, B, 0, 1)
-        proj(1, A, 2)
-        each("g", 0, B, 2, 3)
-        proj(1, A, 3)
-        each("w", 0, B, 0, 1, 2, 3)
-        each("c", 1, A, 0, 1)
-        run("s1", 0, B)
-        each("c", 1, A, 2, 3)
-        run("s2", 0, B)
-        run("stat", 1, B)
-        each("send", 1, A, 4, 5, 6, 7)
-        run("s3", 0, B)
-        run("head", 1, B)
-        proj(1, B, 0, True)
-        proj(1, B, 1, True)
-        wait(("wx", 1))
-        run("x", 1, A)
-        run("norm", 1, B)
-        each("out", 1, B, 0, 1)
-        proj(1, B, 2)
-        each("c", 1, A, 4, 5)
-        proj(1, B, 3)
-        each("send", 1, B, 4, 5, 6, 7)
-        each("c", 1, A, 6, 7)
-        wait(("wdt", 1), ("ss", 1))
-        run("d", 1, A)
-        each("dc", 1, A, 0, 1)
-        each("c", 1, B, 0)
-        each("dc", 1, A, 2, 3)
-        each("c", 1, B, 1, 2, 3)
-        each("y", 1, A, 0, 1, 2, 3)
-        run("ym", 1, A)
-        each("c", 1, B, 4, 5)
-        run("x", 1, B)
-        each("c", 1, B, 6, 7)
-        each("g", 1, A, 0, 1, 2, 3)
-        run("d", 1, B)
-        for c in range(n_c):
-            run("dc", 1, B, c)
-            run("y", 1, B, c)
-        run("ym", 1, B)
-        wait(("wout", 1))
-        each("w", 1, A, 0, 1, 2, 3)
-        each("g", 1, B, 0, 1)
-        run("s1", 1, A)
-        each("w", 1, B, 0)
-        each("g", 1, B, 2)
-        each("w", 1, B, 1)
-        each("g", 1, B, 3)
-        each("w", 1, B, 2, 3)
-        run("s2", 1, A)
-        run("s1", 1, B)
-        run("s3", 1, A)
-        run("s2", 1, B)
-        run("s3", 1, B)
+        run("c", l0, A, X[-1])
+        proj(l0, B, X[-1])
+        run("send", l0, B, Z[0])
+        each("c", l0, A, *Z[:2])
+        run("x", l0, A)
+        each("c", l0, A, *Z[2:])
+        each("c", l0, B, *head2)
+        wait(("wdt", l0), ("ss", l0))
+        run("d", l0, A)
+        each("dc", l0, A, *head2)
+        run("c", l0, B, X[2])
+        each("dc", l0, A, *tail2)
+        run("c", l0, B, X[-1])
+        each("y", l0, A, *X)
+        run("ym", l0, A)
+        each("send", l0, B, *Z[1:])
+        run("c", l0, B, Z[0])
+        each("g", l0, A, *head2)
+        run("x", l0, B)
+        each("g", l0, A, *tail2)
+        each("c", l0, B, *Z[1:3])
+        wait(("wout", l0))
+        each("w", l0, A, *X)
+        run("c", l0, B, Z[-1])
+        run("s1", l0, A)
+        run("d", l0, B)
+        each("dc", l0, B, *X)
+        run("s2", l0, A)
+        run("stat", l1, A)
+        each("y", l0, B, *X)
+        run("ym", l0, B)
+        run("s3", l0, A)
+        wait(*[("win", l1, t) for t in range(n_w)])
+        run("head", l1, A)
+        for c in head2:
+            proj(l1, A, c, True)
+        run("norm", l1, A)
+        each("out", l1, A, *head2)
+        each("g", l0, B, *X)
+        for c in tail2:
+            proj(l1, A, c)
+        each("w", l0, B, *X)
+        each("c", l1, A, *head2)
+        run("s1", l0, B)
+        each("c", l1, A, *tail2)
+        run("s2", l0, B)
+        run("stat", l1, B)
+        each("send", l1, A, *Z)
+        run("s3", l0, B)
+        run("head", l1, B)
+        for c in head2:
+            proj(l1, B, c, True)
+        wait(("wx", l1))
+        run("x", l1, A)
+        run("norm", l1, B)
+        each("out", l1, B, *head2)
+        proj(l1, B, X[2])
+        each("c", l1, A, *Z[:2])
+        proj(l1, B, X[-1])
+        each("c", l1, A, *Z[2:])
+        wait(("wdt", l1), ("ss", l1))
+        run("d", l1, A)
+        each("send", l1, B, *Z[:2])
+        each("dc", l1, A, *head2)
+        run("c", l1, B, X[0])
+        each("send", l1, B, *Z[2:])
+        each("dc", l1, A, *tail2)
+        each("c", l1, B, *X[1:])
+        each("y", l1, A, *X)
+        run("ym", l1, A)
+        each("c", l1, B, *Z[:2])
+        run("x", l1, B)
+        each("c", l1, B, *Z[2:])
+        each("g", l1, A, *X)
+        run("d", l1, B)
+        for c in X:
+            run("dc", l1, B, c)
+            run("y", l1, B, c)
+        run("ym", l1, B)
+        wait(("wout", l1))
+        each("w", l1, A, *X)
+        each("g", l1, B, *head2)
+        run("s1", l1, A)
+        for c in head2:
+            run("w", l1, B, c)
+            run("g", l1, B, c + 2)
+        each("w", l1, B, *tail2)
+        run("s2", l1, A)
+        run("s1", l1, B)
+        run("s3", l1, A)
+        run("s2", l1, B)
+        run("s3", l1, B)
 
         with jax.named_scope("end"):
             all_of(own.at[:, :, :, pl.ds(0, 3)], rs_s, fn_r.at[0, 0, 0]).wait_send()

time: 90.7 us -> 89.5 us (0.987)
  Pallas kernels: 89.5 us -> 88.5 us
    pallas_call x1, Pallas kernels: 85.3 us -> 84.3 us  [local_step(): pl.pallas_call(kernel, out_shape=outs, in_specs=[ANY] * 13, out_specs=(VM...]
where the time goes in v5:
time: 89.5 us; the launch traced here: 89.3 us
  Pallas kernels  88.5 us (99%)
    pallas_call x1, Pallas kernels, local_step(): pl.pallas_call(kernel, out_shape=outs, in_specs=[ANY] * 13, out_specs=(VM...  84.3 us
    pallas_call x1, Pallas kernels, local_step(): pl.pallas_call(store_kernel, out_shape=(jax.ShapeDtypeStruct((rows, d_loc...  4.22 us

profile of v5, /device:TPU:0, one launch (start us, length us, event | category | flops | bytes accessed | tf_op | source)
XLA Modules:
  0.0 89.3 jit_solution(2276449436282549808)
XLA Ops:
  0.6 84.3 %mixer.1 = (f32[2,64,1024]{2,1,0:T(8,128)S(1)}, bf16[2,32,2048]{2,1,0:T(8,128)(2,1)S(1)}, bf16[2,3,32,2048]{3,2,1,0:T(8,128)(2,1)S(1)}, f32[2,32,16,2048]{3,2,1,0:T(8,128)S(1)}) custom-call(f32[128,1024]{1,0:T(8,128)} %r_hbm.1, f32[2,1024]{1,0:T(2,128)} %nw_hbm.1, bf16[2,1024,2,2048]{3,2,1,0:T(2,128)(2,1)} %win_hbm.1, f32[2,4,2048]{2,1,0:T(4,128)} %bitcast.11, ...), custom_call_target="tpu_custom_call" | custom-call | tf_op jit(solution)/shard_map/mixer/pallas_call | solution.py:518
  84.9 4.2 %store.1 = (f32[128,1024]{1,0:T(8,128)}, bf16[2,3,32,2048]{3,2,1,0:T(8,128)(2,1)}, f32[2,32,16,2048]{3,2,1,0:T(8,128)}) custom-call(f32[2,64,1024]{2,1,0:T(8,128)S(1)} %get-tuple-element.10.r, bf16[2,32,2048]{2,1,0:T(8,128)(2,1)S(1)} %get-tuple-element.11.xi, bf16[2,3,32,2048]{3,2,1,0:T(8,128)(2,1)S(1)} %get-tuple-element.12.cs, ...), custom_call_target="tpu_custom_call" | custom-call | tf_op jit(solution)/shard_map/store/pallas_call | solution.py:530

commit v6 on v5

--- a/solution.py
+++ b/solution.py
@@ -514,7 +514,7 @@
         n_layer, _, _, chan = w_in.shape
         rank, n_state = w_dt.shape[1], a_log.shape[-1]
         blk = rows // n_tx
-        kernel, outs, scratch = make_kernel(n_layer, n_tx, n_ty, rows, d_loc, chan, rank, n_state, 512, 2, 2)
+        kernel, outs, scratch = make_kernel(n_layer, n_tx, n_ty, rows, d_loc, chan, rank, n_state, 512, 2, 4)
         parts = pl.pallas_call(
             kernel,
             out_shape=outs,

time: 89.5 us -> 90.2 us (level)
  no operation moved by 1% of the time
where the time goes in v6:
time: 90.2 us; the launch traced here: 90 us
  Pallas kernels  89.2 us (99%)
    pallas_call x1, Pallas kernels, local_step(): pl.pallas_call(kernel, out_shape=outs, in_specs=[ANY] * 13, out_specs=(VM...  85 us
    pallas_call x1, Pallas kernels, local_step(): pl.pallas_call(store_kernel, out_shape=(jax.ShapeDtypeStruct((rows, d_loc...  4.22 us

profile of v6, /device:TPU:0, one launch (start us, length us, event | category | flops | bytes accessed | tf_op | source)
XLA Modules:
  0.0 90.0 jit_solution(9649723854535319699)
XLA Ops:
  0.6 85.0 %mixer.1 = (f32[2,64,1024]{2,1,0:T(8,128)S(1)}, bf16[2,32,2048]{2,1,0:T(8,128)(2,1)S(1)}, bf16[2,3,32,2048]{3,2,1,0:T(8,128)(2,1)S(1)}, f32[2,32,16,2048]{3,2,1,0:T(8,128)S(1)}) custom-call(f32[128,1024]{1,0:T(8,128)} %r_hbm.1, f32[2,1024]{1,0:T(2,128)} %nw_hbm.1, bf16[2,1024,2,2048]{3,2,1,0:T(2,128)(2,1)} %win_hbm.1, f32[2,4,2048]{2,1,0:T(4,128)} %bitcast.11, ...), custom_call_target="tpu_custom_call" | custom-call | tf_op jit(solution)/shard_map/mixer/pallas_call | solution.py:518
  85.6 4.2 %store.1 = (f32[128,1024]{1,0:T(8,128)}, bf16[2,3,32,2048]{3,2,1,0:T(8,128)(2,1)}, f32[2,32,16,2048]{3,2,1,0:T(8,128)}) custom-call(f32[2,64,1024]{2,1,0:T(8,128)S(1)} %get-tuple-element.10.r, bf16[2,32,2048]{2,1,0:T(8,128)(2,1)S(1)} %get-tuple-element.11.xi, bf16[2,3,32,2048]{3,2,1,0:T(8,128)(2,1)S(1)} %get-tuple-element.12.cs, ...), custom_call_target="tpu_custom_call" | custom-call | tf_op jit(solution)/shard_map/store/pallas_call | solution.py:530
